TPU v7x, 32 devices: a whole 2x2x4 slice. The times are simulated.
32 devices in a mesh: img: 4 (over y, core), proj: 8 (over z, x).
Axes of the slice: x: 2, y: 2, z: 4, core: 2. Of those that a mesh axis runs over, the one named last changes fastest.
Arguments:
- images: bfloat16 [512, 4096], P('img'), may hold values from -48 to 48
- projections: bfloat16 [2560, 4096], P('proj'), may hold values from -6 to 6
- noise_weight: float32 [4096], replicated, may hold values from 0.02 to 0.08
- defocus: float32 [512], P('img'), may hold values from 2 to 8
- orient_count: int32 [512], P('img'), may hold values from 160 to 2560, as said below
- term_limit: int32 [512], P('img'), may hold values from 2048 to 4096
- block_plan: int32 [16], replicated, may hold values from 0 to 15, each once
Outputs:
- reconstruction: bfloat16 [2560, 4096], P('proj', 'img')
- evidence_next: float32 [512], P('img')
Inputs may be any that keep to these rules, and one draw needn't show every extreme that they name: Orientations 0 to orient_count[i] - 1 are the significant ones of image i; some image has all 2560.
All inputs are finite; a program needn't handle non-finite values.
Results may differ from a plain program's by a relative error of at most 0.018.
Values may be sent and summed in bfloat16 or wider, within the bound.
A program may use at most 64 MiB of HBM per device.

v0:
```python
import functools
import math

import jax
import jax.numpy as jnp
from jax import lax
from jax.experimental import pallas as pl
from jax.experimental.pallas import tpu as pltpu
from jax.sharding import PartitionSpec as P

BLOCK = 32
PIECES = 2
LANES = 128
MESH = pl.DeviceIdType.MESH
SIN_TERMS = [(-1.0) ** k * math.pi ** (2 * k + 1) / math.factorial(2 * k + 1) for k in range(7)]
COS_TERMS = [(-1.0) ** k * math.pi ** (2 * k) / math.factorial(2 * k) for k in range(8)]


def horner(terms, x):
    total = jnp.full_like(x, terms[-1])
    for term in terms[-2::-1]:
        total = total * x + term
    return total


def sincos_turns(turns):
    rest = turns - jnp.floor(turns + 0.5)
    square = rest * rest
    half_sin = rest * horner(SIN_TERMS, square)
    half_cos = horner(COS_TERMS, square)
    return 2.0 * half_sin * half_cos, 1.0 - 2.0 * half_sin * half_sin


def columns_of(row, rows):
    return jnp.broadcast_to(row, (LANES, rows)).T


def kernel(n_img, n_proj, img_hbm, proj_hbm, noise_hbm, focus_hbm, count_hbm, limit_hbm, plan_hbm,
           rec_ref, ev_ref,
           img, proj, noise_ref, focus_ref, count_ref, limit_ref, plan_ref, weighted, weighted_sq, moved, contrast, back_img, back_wgt, every_post,
           focus_all, limit_all, terms, every_terms, stats, every_stats, scale_out, every_scale,
           load_sem, small_send, small_recv, img_send, img_recv, pass_send, pass_recv, post_send, post_recv,
           stat_send, stat_recv, scale_send, scale_recv):
    me = lax.axis_index("img")
    mine = lax.axis_index("proj")
    img_rows, width = img.shape
    proj_rows = proj.shape[0]
    part = width // n_img
    chips = n_img // 2
    row_y, core = me // 2, lax.rem(me, 2)
    offsets = [(dy, dc) for dy in range(chips - 1, -1, -1) for dc in range(2) if dy or dc]
    img_peers = [lax.rem(row_y + dy, chips) * 2 + lax.rem(core + dc, 2) for dy, dc in offsets]
    img_from = [lax.rem(row_y + chips - dy, chips) * 2 + lax.rem(core + dc, 2) for dy, dc in offsets]
    side = lax.rem(mine, 2)
    beside = mine + 1 - 2 * side
    piece = img_rows // 2 // PIECES
    proj_peers = [lax.rem(mine + k, n_proj) for k in range(1, n_proj)]

    barrier = pltpu.get_barrier_semaphore()
    for peer in img_peers:
        pl.semaphore_signal(barrier, inc=1, device_id={"img": peer}, device_id_type=MESH)
    for peer in proj_peers:
        pl.semaphore_signal(barrier, inc=1, device_id={"proj": peer}, device_id_type=MESH)
    sources = (focus_hbm, limit_hbm, img_hbm, noise_hbm, count_hbm, plan_hbm, proj_hbm)
    targets = (focus_ref, limit_ref, img, noise_ref, count_ref, plan_ref, proj)
    loads = [pltpu.make_async_copy(source, target, load_sem.at[n])
             for n, (source, target) in enumerate(zip(sources, targets))]
    for load in loads:
        load.start()
    loads[0].wait()
    loads[1].wait()

    lane = lax.broadcasted_iota(jnp.int32, (1, LANES), 1).astype(jnp.float32)
    phase = 0.1 / (2.0 * math.pi)
    focus = columns_of(focus_ref[...], img_rows)
    limit = columns_of(limit_ref[...].astype(jnp.float32), img_rows)
    sin0, cos0 = sincos_turns(focus * ((lane + 1.0) / width) + phase)
    sin_d, cos_d = sincos_turns(focus * (LANES / width))

    for load in loads[2:6]:
        load.wait()

    def terms_chunk(c, carry):
        sin_v, cos_v = carry
        cols = pl.ds(pl.multiple_of(c * LANES, LANES), LANES)
        term = lane + (c * LANES).astype(jnp.float32)
        kept = jnp.where(term < limit, sin_v, 0.0)
        noisy = kept * noise_ref[:, cols]
        weighted[:, cols] = (noisy * img[:, cols].astype(jnp.float32)).astype(jnp.bfloat16)
        weighted_sq[:, cols] = (noisy * (-0.5 * sin_v)).astype(jnp.bfloat16)
        return sin_v * cos_d + cos_v * sin_d, cos_v * cos_d - sin_v * sin_d

    lax.fori_loop(0, width // LANES, terms_chunk, (sin0, cos0), unroll=2)
    loads[6].wait()

    depth = 512
    contract = (((1,), (1,)), ((), ()))

    def score_chunk(c, total):
        cols = pl.ds(pl.multiple_of(c * depth, depth), depth)
        rows = proj[:, cols]
        total = total + lax.dot_general(rows, weighted[:, cols], contract, preferred_element_type=jnp.float32)
        return total + lax.dot_general(rows * rows, weighted_sq[:, cols], contract,
                                       preferred_element_type=jnp.float32)

    scores = lax.fori_loop(0, width // depth, score_chunk, jnp.zeros((proj_rows, img_rows), jnp.float32))

    orient = lax.broadcasted_iota(jnp.int32, (proj_rows, img_rows), 0) + mine * proj_rows
    significant = orient < count_ref[...]
    peak = jnp.max(jnp.where(significant, scores, -1e30), axis=0, keepdims=True)
    expo = jnp.where(significant, jnp.exp(jnp.where(significant, scores - peak, 0.0)), 0.0)
    mass = jnp.sum(expo, axis=0, keepdims=True)
    stats[0:1, :] = peak
    stats[1:2, :] = mass
    terms[...] = expo.astype(jnp.bfloat16)

    pl.semaphore_wait(barrier, n_img + n_proj - 2)

    small = []
    for k, peer in enumerate(img_peers):
        for t, (ref, dst) in enumerate(((focus_ref, focus_all), (limit_ref, limit_all))):
            small.append(pltpu.make_async_remote_copy(
                src_ref=ref, dst_ref=dst.at[me], send_sem=small_send.at[t, k],
                recv_sem=small_recv.at[t, k], device_id={"img": peer}, device_id_type=MESH))
            small[-1].start()
    stat_copies = []
    for k, peer in enumerate(proj_peers):
        stat_copies.append(pltpu.make_async_remote_copy(
            src_ref=stats, dst_ref=every_stats.at[mine], send_sem=stat_send.at[k],
            recv_sem=stat_recv.at[k], device_id={"proj": peer}, device_id_type=MESH))
        stat_copies[-1].start()
    moves = []
    for k, peer in enumerate(img_peers):
        slab = pl.ds(pl.multiple_of(peer * part, LANES), part)
        if offsets[k][0]:
            for n in range(PIECES):
                rows = pl.ds(pl.multiple_of((side * PIECES + n) * piece, piece), piece)
                moves.append((k, n, pltpu.make_async_remote_copy(
                    src_ref=img.at[rows, slab], dst_ref=moved.at[me, rows, :], send_sem=img_send.at[k, n],
                    recv_sem=img_recv.at[k, n], device_id={"img": peer}, device_id_type=MESH)))
        else:
            near = pltpu.make_async_remote_copy(
                src_ref=img.at[:, slab], dst_ref=moved.at[me], send_sem=img_send.at[k, 0],
                recv_sem=img_recv.at[k, 0], device_id={"img": peer}, device_id_type=MESH)
    for _, _, copy in moves:
        copy.start()
    near.start()
    post_copies = []
    for k, peer in enumerate(img_peers):
        post_copies.append(pltpu.make_async_remote_copy(
            src_ref=terms, dst_ref=every_terms.at[me], send_sem=post_send.at[k],
            recv_sem=post_recv.at[k], device_id={"img": peer}, device_id_type=MESH))
        post_copies[-1].start()

    for copy in small:
        copy.wait()
    focus_all[me] = focus_ref[...]
    limit_all[me] = limit_ref[...]
    start = (me * part).astype(jnp.float32)
    term0 = lane + start

    def weights_block(b, carry):
        focus_b = columns_of(focus_all[b], img_rows)
        limit_b = columns_of(limit_all[b].astype(jnp.float32), img_rows)
        sin_v, cos_v = sincos_turns(focus_b * ((term0 + 1.0) / width) + phase)
        sin_b, cos_b = sincos_turns(focus_b * (LANES / width))
        rows = pl.ds(pl.multiple_of(b * img_rows, img_rows), img_rows)
        for c in range(part // LANES):
            cols = slice(c * LANES, (c + 1) * LANES)
            kept = jnp.where(term0 + float(c * LANES) < limit_b, sin_v, 0.0)
            contrast[rows, cols] = kept
            back_wgt[rows, cols] = (kept * sin_v).astype(jnp.bfloat16)
            sin_v, cos_v = sin_v * cos_b + cos_v * sin_b, cos_v * cos_b - sin_v * sin_b
        return carry

    lax.fori_loop(0, n_img, weights_block, 0)

    every_stats[mine] = stats[...]
    for copy in stat_copies:
        copy.wait()
    peaks = [every_stats[q, 0:1, :] for q in range(n_proj)]
    top = functools.reduce(jnp.maximum, peaks)
    whole = sum(every_stats[q, 1:2, :] * jnp.exp(peaks[q] - top) for q in range(n_proj))
    evidence = top + jnp.log(whole)
    scale_out[0:1, :] = jnp.exp(peak - evidence)
    scale_out[1:2, :] = evidence
    scale_copies = []
    for k, peer in enumerate(img_peers):
        scale_copies.append(pltpu.make_async_remote_copy(
            src_ref=scale_out, dst_ref=every_scale.at[me], send_sem=scale_send.at[k],
            recv_sem=scale_recv.at[k], device_id={"img": peer}, device_id_type=MESH))
        scale_copies[-1].start()
    every_scale[me] = scale_out[...]

    def take_images(b, pixels):
        rows = pl.ds(pl.multiple_of(b * img_rows, img_rows), img_rows)
        back_img[rows, :] = (contrast[rows, :] * pixels.astype(jnp.float32)).astype(jnp.bfloat16)

    def take_post(b, values):
        cols = pl.ds(pl.multiple_of(b * img_rows, img_rows), img_rows)
        every_post[:, cols] = (values.astype(jnp.float32) * every_scale[b][0:1, :]).astype(jnp.bfloat16)

    take_images(me, img[:, pl.ds(pl.multiple_of(me * part, LANES), part)])
    every_post[:, pl.ds(pl.multiple_of(me * img_rows, img_rows), img_rows)] = (
        expo * every_scale[me][0:1, :]).astype(jnp.bfloat16)
    near.wait()
    take_images(img_from[-1], moved[img_from[-1]])
    passed = []
    for k, n, copy in moves:
        copy.wait()
        held = moved.at[img_from[k], pl.ds(pl.multiple_of((side * PIECES + n) * piece, piece), piece), :]
        passed.append(pltpu.make_async_remote_copy(
            src_ref=held, dst_ref=held, send_sem=pass_send.at[k, n], recv_sem=pass_recv.at[k, n],
            device_id={"proj": beside}, device_id_type=MESH))
        passed[-1].start()
    for k, source in enumerate(img_from):
        post_copies[k].wait()
        scale_copies[k].wait()
        take_post(source, every_terms[source])
    for copy in passed:
        copy.wait()
    for source in img_from[:-1]:
        take_images(source, moved[source])

    step = min(part, 256)
    posts = every_post[...]
    for c in range(part // step):
        cols = slice(c * step, (c + 1) * step)
        sums = jnp.dot(posts, back_img[:, cols], preferred_element_type=jnp.float32)
        weights = jnp.dot(posts, back_wgt[:, cols], preferred_element_type=jnp.float32)
        rec_ref[:, cols] = (sums / (weights + 1.0)).astype(jnp.bfloat16)

    groups = img_rows // BLOCK
    group = lax.broadcasted_iota(jnp.int32, (1, img_rows), 1) // BLOCK
    placed = jnp.zeros((1, img_rows), jnp.float32)
    for a in range(n_img):
        plan = jnp.zeros((1, img_rows), jnp.int32)
        for g in range(groups):
            plan = jnp.where(group == g, plan_ref[a * groups + g], plan)
        values = every_scale[a][1:2, :]
        for t in range(groups):
            turned, target = values, plan
            if t:
                turned = pltpu.roll(values, t * BLOCK, 1)
                target = pltpu.roll(plan, t * BLOCK, 1)
            placed = placed + jnp.where(target == me * groups + group, turned, 0.0)
    ev_ref[...] = placed


def shards(n_img, n_proj, images, projections, noise_weight, defocus, orient_count, term_limit, block_plan):
    img_rows, width = images.shape
    proj_rows = projections.shape[0]
    part = width // n_img
    vmem = pl.BlockSpec(memory_space=pltpu.VMEM)
    hbm = pl.BlockSpec(memory_space=pl.ANY)
    bf16, f32 = jnp.bfloat16, jnp.float32
    dma = pltpu.SemaphoreType.DMA
    reconstruction, evidence = pl.pallas_call(
        functools.partial(kernel, n_img, n_proj),
        out_shape=(jax.ShapeDtypeStruct((proj_rows, part), bf16), jax.ShapeDtypeStruct((1, img_rows), f32)),
        in_specs=[hbm] * 7,
        out_specs=(vmem, vmem),
        scratch_shapes=[
            pltpu.VMEM((img_rows, width), bf16),
            pltpu.VMEM((proj_rows, width), bf16),
            pltpu.VMEM((1, width), f32),
            pltpu.VMEM((1, img_rows), f32),
            pltpu.VMEM((1, img_rows), jnp.int32),
            pltpu.VMEM((1, img_rows), jnp.int32),
            pltpu.SMEM(block_plan.shape, jnp.int32),
            pltpu.VMEM((img_rows, width), bf16),
            pltpu.VMEM((img_rows, width), bf16),
            pltpu.VMEM((n_img, img_rows, part), bf16),
            pltpu.VMEM((n_img * img_rows, part), f32),
            pltpu.VMEM((n_img * img_rows, part), bf16),
            pltpu.VMEM((n_img * img_rows, part), bf16),
            pltpu.VMEM((proj_rows, n_img * img_rows), bf16),
            pltpu.VMEM((n_img, 1, img_rows), f32),
            pltpu.VMEM((n_img, 1, img_rows), jnp.int32),
            pltpu.VMEM((proj_rows, img_rows), bf16),
            pltpu.VMEM((n_img, proj_rows, img_rows), bf16),
            pltpu.VMEM((2, img_rows), f32),
            pltpu.VMEM((n_proj, 2, img_rows), f32),
            pltpu.VMEM((2, img_rows), f32),
            pltpu.VMEM((n_img, 2, img_rows), f32),
            dma((7,)),
            dma((2, n_img)), dma((2, n_img)),
            dma((n_img, PIECES)), dma((n_img, PIECES)),
            dma((n_img, PIECES)), dma((n_img, PIECES)),
            dma((n_img,)), dma((n_img,)),
            dma((n_proj,)), dma((n_proj,)),
            dma((n_img,)), dma((n_img,)),
        ],
        compiler_params=pltpu.CompilerParams(
            collective_id=0, has_side_effects=True, vmem_limit_bytes=62 * 1024 * 1024),
    )(images, projections, noise_weight.reshape(1, -1), defocus.reshape(1, -1), orient_count.reshape(1, -1),
      term_limit.reshape(1, -1), block_plan)
    return reconstruction, evidence.reshape(-1)


def solution(mesh):
    n_img, n_proj = mesh.shape["img"], mesh.shape["proj"]
    placed = (P("img", None), P("proj", None), P(), P("img"), P("img"), P("img"), P())
    return jax.shard_map(
        functools.partial(shards, n_img, n_proj), mesh=mesh, in_specs=placed,
        out_specs=(P("proj", "img"), P("img")), check_vma=False,
    )
```

profile of v0, /device:TPU:0, one launch (start us, length us, event | category | flops | bytes accessed | tf_op | source)
XLA Modules:
  0.0 26.2 jit_solution(3945047810210811608)
XLA Ops:
  0.6 22.4 %shard_map.86 = (bf16[320,1024]{1,0:T(8,128)(2,1)}, f32[1,128]{1,0:T(1,128)}) custom-call(bf16[128,4096]{1,0:T(8,128)(2,1)} %img_hbm.1, bf16[320,4096]{1,0:T(8,128)(2,1)} %proj_hbm.1, f32[1,4096]{1,0:T(1,128)} %bitcast.5, f32[1,128]{1,0:T(1,128)} %bitcast.6, s32[1,128]{1,0:T(1,128)} %bitcast.7, s32[1,128]{1,0:T(1,128)} %bitcast.8, s32[16]{0:T(128)} %plan_hbm.1), custom_call_target="tpu_custom_call" | custom-call | tf_op jit(solution)/shard_map/pallas_call | solution.py:258
  23.1 2.0 %copy.11 = bf16[320,1024]{1,0:T(8,128)(2,1)} copy(bf16[320,1024]{1,0:T(8,128)(2,1)} %get-tuple-element.8) | data formatting | bytes 1310720
  25.0 1.2 %copy.12 = f32[128]{0:T(128)} copy(f32[128]{0:T(128)} %bitcast.9) | data formatting | bytes 1024
where the time goes:
time: 26.4 us; the launch traced here: 26.2 us
  Pallas kernels  22.4 us (85%)
  local copies, waits for them, and re-layouts  3.13 us (12%)
  between operations  0.64 us (2%)
    pallas_call x1, Pallas kernels, shards(): pl.pallas_call(functools.partial(kernel, n_img, n_proj), out_shape=(jax.S...  22.4 us
    unnamed x2, local copies, waits for them, and re-layouts  3.13 us

commit v1 on v0

v1 whole, which is shorter than its diff:
```python
import functools
import math

import jax
import jax.numpy as jnp
from jax import lax
from jax.experimental import pallas as pl
from jax.experimental.pallas import tpu as pltpu
from jax.sharding import PartitionSpec as P

BLOCK = 32
PIECES = 2
LANES = 128
DEPTH = 512
LOADS = 4
MESH = pl.DeviceIdType.MESH
SIN_TERMS = [(-1.0) ** k * math.pi ** (2 * k + 1) / math.factorial(2 * k + 1) for k in range(7)]
COS_TERMS = [(-1.0) ** k * math.pi ** (2 * k) / math.factorial(2 * k) for k in range(8)]


def horner(terms, x):
    total = jnp.full_like(x, terms[-1])
    for term in terms[-2::-1]:
        total = total * x + term
    return total


def sincos_turns(turns):
    rest = turns - jnp.floor(turns + 0.5)
    square = rest * rest
    half_sin = rest * horner(SIN_TERMS, square)
    half_cos = horner(COS_TERMS, square)
    return 2.0 * half_sin * half_cos, 1.0 - 2.0 * half_sin * half_sin


def columns_of(row, rows):
    return jnp.broadcast_to(row, (LANES, rows)).T


def sine_start(focus, term0, width):
    sin0, cos0 = sincos_turns(focus * ((term0 + 1.0) / width) + 0.1 / (2.0 * math.pi))
    sin_d, cos_d = sincos_turns(focus * (LANES / width))
    return sin0, sin0 * cos_d - cos0 * sin_d, 2.0 * cos_d


def wait_bytes(ref, sem):
    pltpu.make_async_copy(ref, ref, sem).wait()


def score_kernel(n_img, n_proj, x_size, img_hbm, proj_hbm, noise_hbm, focus_hbm, count_hbm, limit_hbm, plan_hbm,
                 posts_ref, back_img, back_wgt, ev_ref,
                 img, proj, noise_ref, focus_ref, count_ref, limit_ref, plan_ref, weighted, weighted_sq, total,
                 moved, contrast, focus_all, limit_all, terms, every_terms, stats, every_stats,
                 load_sem, img_load, proj_load, x_token, up_token, down_token,
                 small_send, small_recv, img_send, img_recv, pass_send, pass_recv,
                 post_send, post_recv, stat_send, stat_recv):
    me = lax.axis_index("img")
    mine = lax.axis_index("proj")
    img_rows, width = img.shape
    proj_rows = proj.shape[0]
    part = width // n_img
    chips = n_img // 2
    z_size = n_proj // x_size
    row_y, core = me // 2, lax.rem(me, 2)
    at_x, at_z = lax.rem(mine, x_size), mine // x_size

    def img_to(t):
        return lax.rem(row_y + t // 2, chips) * 2 + lax.rem(core + t % 2, 2)

    def img_from(t):
        return lax.rem(row_y + chips - t // 2, chips) * 2 + lax.rem(core + t % 2, 2)

    side = lax.rem(mine, 2)
    beside = mine + 1 - 2 * side
    piece = img_rows // 2 // PIECES
    x_peers = [at_z * x_size + lax.rem(at_x + k, x_size) for k in range(1, x_size)]
    bottom, top = at_z == 0, at_z == z_size - 1

    barrier = pltpu.get_barrier_semaphore()
    for t in range(1, n_img):
        pl.semaphore_signal(barrier, inc=1, device_id={"img": img_to(t)}, device_id_type=MESH)
    for peer in x_peers:
        pl.semaphore_signal(barrier, inc=1, device_id={"proj": peer}, device_id_type=MESH)

    def signal_up(sem):
        pl.semaphore_signal(sem, inc=1, device_id={"proj": mine + x_size}, device_id_type=MESH)

    def signal_down(sem):
        pl.semaphore_signal(sem, inc=1, device_id={"proj": mine - x_size}, device_id_type=MESH)

    pl.when(jnp.logical_not(top))(lambda: signal_up(barrier))
    pl.when(jnp.logical_not(bottom))(lambda: signal_down(barrier))

    small_loads = [pltpu.make_async_copy(source, target, load_sem.at[n]) for n, (source, target) in enumerate(
        ((focus_hbm, focus_ref), (limit_hbm, limit_ref), (noise_hbm, noise_ref), (count_hbm, count_ref),
         (plan_hbm, plan_ref)))]
    wide = width // LOADS
    img_loads = [pltpu.make_async_copy(img_hbm.at[:, pl.ds(n * wide, wide)], img.at[:, pl.ds(n * wide, wide)],
                                       img_load.at[n]) for n in range(LOADS)]
    proj_loads = [pltpu.make_async_copy(proj_hbm.at[:, pl.ds(n * wide, wide)], proj.at[:, pl.ds(n * wide, wide)],
                                        proj_load.at[n]) for n in range(LOADS)]
    for load in small_loads[:3]:
        load.start()
    for n in range(LOADS):
        img_loads[n].start()
        proj_loads[n].start()
    for load in small_loads[3:]:
        load.start()
    small_loads[0].wait()
    small_loads[1].wait()

    lane = lax.broadcasted_iota(jnp.int32, (1, LANES), 1).astype(jnp.float32)
    focus = columns_of(focus_ref[...], img_rows)
    limit = columns_of(limit_ref[...].astype(jnp.float32), img_rows)
    sin_v, sin_before, turn = sine_start(focus, lane, width)
    small_loads[2].wait()
    contract = (((1,), (1,)), ((), ()))
    small, moves = [], []

    def terms_chunk(c, sin_v, sin_before):
        for k in range(DEPTH // LANES):
            first = c * DEPTH + k * LANES
            cols = slice(first, first + LANES)
            kept = jnp.where(lane + float(first) < limit, sin_v, 0.0)
            noisy = kept * noise_ref[:, cols]
            weighted[:, cols] = (noisy * img[:, cols].astype(jnp.float32)).astype(jnp.bfloat16)
            weighted_sq[:, cols] = (noisy * (-0.5 * sin_v)).astype(jnp.bfloat16)
            sin_v, sin_before = turn * sin_v - sin_before, sin_v
        return sin_v, sin_before

    def score_chunk(c):
        cols = slice(c * DEPTH, (c + 1) * DEPTH)
        rows = proj[:, cols]
        got = lax.dot_general(rows, weighted[:, cols], contract, preferred_element_type=jnp.float32)
        got = got + lax.dot_general(rows * rows, weighted_sq[:, cols], contract, preferred_element_type=jnp.float32)
        if c:
            total[...] += got
        else:
            total[...] = got

    def start_img(n):
        for t in range(2, n_img):
            rows = pl.ds(pl.multiple_of((side * PIECES + n) * piece, piece), piece)
            slab = pl.ds(pl.multiple_of(img_to(t) * part, LANES), part)
            copy = pltpu.make_async_remote_copy(
                src_ref=img.at[rows, slab], dst_ref=moved.at[t, rows, :], send_sem=img_send.at[t, n],
                recv_sem=img_recv.at[t, n], device_id={"img": img_to(t)}, device_id_type=MESH)
            copy.start()
            moves.append((t, n, copy))

    chunks = width // DEPTH
    per_load = wide // DEPTH
    loaded = []

    def need_img(n):
        for k in range(len(loaded), n + 1):
            img_loads[k].wait()
            loaded.append(k)

    need_img(0)
    sin_v, sin_before = terms_chunk(0, sin_v, sin_before)
    near = None
    for c in range(chunks):
        if c + 1 < chunks:
            need_img((c + 1) // per_load)
            sin_v, sin_before = terms_chunk(c + 1, sin_v, sin_before)
        if c % per_load == 0:
            proj_loads[c // per_load].wait()
        score_chunk(c)
        if c == (chunks // 4 if chunks >= 8 else 0):
            pl.semaphore_wait(barrier, n_img + x_size - 2 + jnp.where(bottom, 0, 1) + jnp.where(top, 0, 1))
            for peer in x_peers:
                pl.semaphore_signal(x_token, inc=1, device_id={"proj": peer}, device_id_type=MESH)
            for t in range(1, n_img):
                for n, (ref, dst) in enumerate(((focus_ref, focus_all), (limit_ref, limit_all))):
                    small.append(pltpu.make_async_remote_copy(
                        src_ref=ref, dst_ref=dst.at[t], send_sem=small_send.at[n, t], recv_sem=small_recv.at[n, t],
                        device_id={"img": img_to(t)}, device_id_type=MESH))
                    small[-1].start()
        if c == chunks // 2:
            need_img(LOADS - 1)
            start_img(0)
            near = pltpu.make_async_remote_copy(
                src_ref=img.at[:, pl.ds(pl.multiple_of(img_to(1) * part, LANES), part)], dst_ref=moved.at[1],
                send_sem=img_send.at[1, 0], recv_sem=img_recv.at[1, 0], device_id={"img": img_to(1)},
                device_id_type=MESH)
            near.start()
            pl.semaphore_wait(x_token, x_size - 1)
            pl.when(bottom)(lambda: signal_up(up_token))
            pl.when(top)(lambda: signal_down(down_token))
            for n in range(1, PIECES):
                start_img(n)
        if c == chunks * 3 // 4:
            @pl.when(jnp.logical_not(bottom))
            def _():
                pl.semaphore_wait(up_token, 1)
                pl.when(jnp.logical_not(top))(lambda: signal_up(up_token))

    small_loads[3].wait()
    small_loads[4].wait()
    scores = total[...]
    orient = lax.broadcasted_iota(jnp.int32, (proj_rows, img_rows), 0) + mine * proj_rows
    significant = orient < count_ref[...]
    masked = jnp.where(significant, scores, -1e30)
    peak = jnp.max(masked, axis=0, keepdims=True)
    expo = jnp.where(significant, jnp.exp(masked - peak), 0.0)
    stats[0:1, :] = peak
    stats[1:2, :] = jnp.sum(expo, axis=0, keepdims=True)
    terms[...] = expo.astype(jnp.bfloat16)

    @pl.when(jnp.logical_not(top))
    def _():
        pl.semaphore_wait(down_token, 1)
        pl.when(jnp.logical_not(bottom))(lambda: signal_down(down_token))

    def send_stats(n, carry):
        t, j = n // n_proj, lax.rem(n, n_proj)
        pltpu.make_async_remote_copy(
            src_ref=stats, dst_ref=every_stats.at[n], send_sem=stat_send, recv_sem=stat_recv,
            device_id={"img": lax.rem(row_y + t // 2, chips) * 2 + lax.rem(core + lax.rem(t, 2), 2),
                       "proj": lax.rem(mine + j, n_proj)}, device_id_type=MESH).start()
        return carry

    lax.fori_loop(1, n_img * n_proj, send_stats, 0)
    post_copies = [pltpu.make_async_remote_copy(
        src_ref=terms, dst_ref=every_terms.at[t], send_sem=post_send.at[t], recv_sem=post_recv.at[t],
        device_id={"img": img_to(t)}, device_id_type=MESH) for t in range(1, n_img)]
    for copy in post_copies[::-1]:
        copy.start()

    term0 = lane + (me * part).astype(jnp.float32)

    def weights_block(t, focus_row, limit_row):
        limit_b = columns_of(limit_row.astype(jnp.float32), img_rows)
        sin_v, sin_before, turn = sine_start(columns_of(focus_row, img_rows), term0, width)
        rows = pl.ds(pl.multiple_of(t * img_rows, img_rows), img_rows)
        for c in range(part // LANES):
            cols = slice(c * LANES, (c + 1) * LANES)
            kept = jnp.where(term0 + float(c * LANES) < limit_b, sin_v, 0.0)
            contrast[rows, cols] = kept
            back_wgt[rows, cols] = (kept * sin_v).astype(jnp.bfloat16)
            sin_v, sin_before = turn * sin_v - sin_before, sin_v

    def take_images(t, pixels):
        rows = pl.ds(t * img_rows, img_rows)
        back_img[rows, :] = (contrast[rows, :] * pixels.astype(jnp.float32)).astype(jnp.bfloat16)

    focus_all[0] = focus_ref[...]
    limit_all[0] = limit_ref[...]
    for copy in small:
        copy.wait()

    def any_block(t, carry):
        weights_block(t, focus_all[t], limit_all[t])
        return carry

    lax.fori_loop(0, n_img, any_block, 0)
    passed = []

    def pass_on(t, n, copy):
        copy.wait()
        held = moved.at[t, pl.ds(pl.multiple_of((side * PIECES + n) * piece, piece), piece), :]
        passed.append(pltpu.make_async_remote_copy(
            src_ref=held, dst_ref=held, send_sem=pass_send.at[t, n], recv_sem=pass_recv.at[t, n],
            device_id={"proj": beside}, device_id_type=MESH))
        passed[-1].start()

    for move in moves[:n_img - 2]:
        pass_on(*move)
    take_images(0, img[:, pl.ds(pl.multiple_of(me * part, LANES), part)])
    near.wait()
    take_images(1, moved[1])
    for move in moves[n_img - 2:]:
        pass_on(*move)
    for copy in passed:
        copy.wait()
    for t in range(2, n_img):
        take_images(t, moved[t])

    every_stats[0] = stats[...]
    wait_bytes(every_stats.at[pl.ds(1, n_img * n_proj - 1)], stat_recv)
    wait_bytes(every_stats.at[pl.ds(1, n_img * n_proj - 1)], stat_send)
    evidence = []
    for t in range(n_img):
        every = every_stats[pl.ds(t * n_proj, n_proj)]
        peaks, masses = every[:, 0, :], every[:, 1, :]
        highest = jnp.max(peaks, axis=0, keepdims=True)
        whole = jnp.sum(masses * jnp.exp(peaks - highest), axis=0, keepdims=True)
        evidence.append(highest + jnp.log(whole))
        scale = jnp.exp(peaks[0:1, :] - evidence[t])
        if t:
            post_copies[t - 1].wait()
        values = every_terms[t].astype(jnp.float32) if t else expo
        posts_ref[:, t * img_rows:(t + 1) * img_rows] = (values * scale).astype(jnp.bfloat16)

    groups = img_rows // BLOCK
    group = lax.broadcasted_iota(jnp.int32, (1, img_rows), 1) // BLOCK
    placed = jnp.zeros((1, img_rows), jnp.float32)
    for t in range(n_img):
        plan = jnp.zeros((1, img_rows), jnp.int32)
        for g in range(groups):
            plan = jnp.where(group == g, plan_ref[img_from(t) * groups + g], plan)
        for s in range(groups):
            turned, target = evidence[t], plan
            if s:
                turned = pltpu.roll(evidence[t], s * BLOCK, 1)
                target = pltpu.roll(plan, s * BLOCK, 1)
            placed = placed + jnp.where(target == me * groups + group, turned, 0.0)
    ev_ref[...] = placed


def back_kernel(posts_ref, back_img, back_wgt, ev_ref, rec_hbm, placed_hbm, rec, out_sem):
    part = back_img.shape[1]
    step = min(part, 256)
    steps = part // step
    posts = posts_ref[...]
    last = pltpu.make_async_copy(ev_ref, placed_hbm, out_sem.at[steps])
    last.start()
    copies = [last]
    for c in range(steps):
        cols = slice(c * step, (c + 1) * step)
        sums = jnp.dot(posts, back_img[:, cols], preferred_element_type=jnp.float32)
        weights = jnp.dot(posts, back_wgt[:, cols], preferred_element_type=jnp.float32)
        rec[:, cols] = (sums / (weights + 1.0)).astype(jnp.bfloat16)
        copies.append(pltpu.make_async_copy(rec.at[:, cols], rec_hbm.at[:, cols], out_sem.at[c]))
        copies[-1].start()
    for copy in copies:
        copy.wait()


def shards(n_img, n_proj, images, projections, noise_weight, defocus, orient_count, term_limit, block_plan):
    img_rows, width = images.shape
    proj_rows = projections.shape[0]
    part = width // n_img
    x_size = 1 << ((n_proj.bit_length() - 1) // 2)
    vmem = pl.BlockSpec(memory_space=pltpu.VMEM)
    hbm = pl.BlockSpec(memory_space=pl.ANY)
    bf16, f32, i32 = jnp.bfloat16, jnp.float32, jnp.int32
    dma, regular = pltpu.SemaphoreType.DMA, pltpu.SemaphoreType.REGULAR
    held = pl.pallas_call(
        functools.partial(score_kernel, n_img, n_proj, x_size),
        out_shape=(pltpu.VMEM((proj_rows, n_img * img_rows), bf16), pltpu.VMEM((n_img * img_rows, part), bf16),
                   pltpu.VMEM((n_img * img_rows, part), bf16), pltpu.VMEM((1, img_rows), f32)),
        in_specs=[hbm] * 7,
        out_specs=(vmem, vmem, vmem, vmem),
        scratch_shapes=[
            pltpu.VMEM((img_rows, width), bf16),
            pltpu.VMEM((proj_rows, width), bf16),
            pltpu.VMEM((1, width), f32),
            pltpu.VMEM((1, img_rows), f32),
            pltpu.VMEM((1, img_rows), i32),
            pltpu.VMEM((1, img_rows), i32),
            pltpu.SMEM(block_plan.shape, i32),
            pltpu.VMEM((img_rows, width), bf16),
            pltpu.VMEM((img_rows, width), bf16),
            pltpu.VMEM((proj_rows, img_rows), f32),
            pltpu.VMEM((n_img, img_rows, part), bf16),
            pltpu.VMEM((n_img * img_rows, part), f32),
            pltpu.VMEM((n_img, 1, img_rows), f32),
            pltpu.VMEM((n_img, 1, img_rows), i32),
            pltpu.VMEM((proj_rows, img_rows), bf16),
            pltpu.VMEM((n_img, proj_rows, img_rows), bf16),
            pltpu.VMEM((2, img_rows), f32),
            pltpu.VMEM((n_img * n_proj, 2, img_rows), f32),
            dma((5,)), dma((LOADS,)), dma((LOADS,)), regular, regular, regular,
            dma((2, n_img)), dma((2, n_img)),
            dma((n_img, PIECES)), dma((n_img, PIECES)),
            dma((n_img, PIECES)), dma((n_img, PIECES)),
            dma((n_img,)), dma((n_img,)), dma, dma,
        ],
        compiler_params=pltpu.CompilerParams(
            collective_id=0, has_side_effects=True, vmem_limit_bytes=54 * 1024 * 1024),
    )(images, projections, noise_weight.reshape(1, -1), defocus.reshape(1, -1), orient_count.reshape(1, -1),
      term_limit.reshape(1, -1), block_plan)
    reconstruction, evidence = pl.pallas_call(
        back_kernel,
        out_shape=(jax.ShapeDtypeStruct((proj_rows, part), bf16), jax.ShapeDtypeStruct((1, img_rows), f32)),
        in_specs=[vmem] * 4,
        out_specs=(hbm, hbm),
        scratch_shapes=[pltpu.VMEM((proj_rows, part), bf16), dma((part // min(part, 256) + 1,))],
        compiler_params=pltpu.CompilerParams(vmem_limit_bytes=16 * 1024 * 1024),
    )(*held)
    return reconstruction, evidence.reshape(-1)


def solution(mesh):
    n_img, n_proj = mesh.shape["img"], mesh.shape["proj"]
    placed = (P("img", None), P("proj", None), P(), P("img"), P("img"), P("img"), P())
    return jax.shard_map(
        functools.partial(shards, n_img, n_proj), mesh=mesh, in_specs=placed,
        out_specs=(P("proj", "img"), P("img")), check_vma=False,
    )
```

time: 26.4 us -> 23 us (0.87)
  local copies, waits for them, and re-layouts: 3.13 us -> 0 us
    unnamed x2 -> x0, local copies, waits for them, and re-layouts: 3.13 us -> none
    pallas_call x1 -> x2, Pallas kernels: 22.4 us -> 22.2 us  [the longest x1 20.6 us: shards(): pl.pallas_call(functools.partial(score_kernel, n_img, n_proj, x_size), ou...]
where the time goes in v1:
time: 23 us; the launch traced here: 22.9 us
  Pallas kernels  22.2 us (97%)
  between operations  0.64 us (3%)
    pallas_call x1, Pallas kernels, shards(): pl.pallas_call(functools.partial(score_kernel, n_img, n_proj, x_size), ou...  20.6 us
    pallas_call x1, Pallas kernels, shards(): pl.pallas_call(back_kernel, out_shape=(jax.ShapeDtypeStruct((proj_rows, p...  1.58 us

profile of v1, /device:TPU:0, one launch (start us, length us, event | category | flops | bytes accessed | tf_op | source)
XLA Modules:
  0.0 22.9 jit_solution(9777044399747072722)
XLA Ops:
  0.6 20.6 %shard_map.86 = (bf16[320,512]{1,0:T(8,128)(2,1)S(1)}, bf16[512,1024]{1,0:T(8,128)(2,1)S(1)}, bf16[512,1024]{1,0:T(8,128)(2,1)S(1)}, f32[1,128]{1,0:T(1,128)S(1)}) custom-call(bf16[128,4096]{1,0:T(8,128)(2,1)} %img_hbm.1, bf16[320,4096]{1,0:T(8,128)(2,1)} %proj_hbm.1, f32[1,4096]{1,0:T(1,128)} %bitcast.5, f32[1,128]{1,0:T(1,128)} %bitcast.6, ...), custom_call_target="tpu_custom_call" | custom-call | tf_op jit(solution)/shard_map/pallas_call | solution.py:340
  21.3 1.6 %shard_map.87 = (bf16[320,1024]{1,0:T(8,128)(2,1)}, f32[1,128]{1,0:T(1,128)}) custom-call(bf16[320,512]{1,0:T(8,128)(2,1)S(1)} %get-tuple-element.8.posts_ref, bf16[512,1024]{1,0:T(8,128)(2,1)S(1)} %get-tuple-element.9.back_img, bf16[512,1024]{1,0:T(8,128)(2,1)S(1)} %get-tuple-element.10.back_wgt, f32[1,128]{1,0:T(1,128)S(1)} %get-tuple-element.11.ev_ref), custom_call_target="tpu_custom_call" | custom-call | tf_op jit(solution)/shard_map/pallas_call | solution.py:375

commit v2 on v1

v2 whole, which is shorter than its diff:
```python
import functools
import math

import jax
import jax.numpy as jnp
from jax import lax
from jax.experimental import pallas as pl
from jax.experimental.pallas import tpu as pltpu
from jax.sharding import PartitionSpec as P

BLOCK = 32
PIECES = 4
LANES = 128
DEPTH = 512
NEAR_STEP = 1
MESH = pl.DeviceIdType.MESH
SIN_TERMS = [(-1.0) ** k * math.pi ** (2 * k + 1) / math.factorial(2 * k + 1) for k in range(7)]
COS_TERMS = [(-1.0) ** k * math.pi ** (2 * k) / math.factorial(2 * k) for k in range(8)]


def horner(terms, x):
    total = jnp.full_like(x, terms[-1])
    for term in terms[-2::-1]:
        total = total * x + term
    return total


def sincos_turns(turns):
    rest = turns - jnp.floor(turns + 0.5)
    square = rest * rest
    half_sin = rest * horner(SIN_TERMS, square)
    half_cos = horner(COS_TERMS, square)
    return 2.0 * half_sin * half_cos, 1.0 - 2.0 * half_sin * half_sin


def columns_of(row, rows):
    return jnp.broadcast_to(row, (LANES, rows)).T


def step_sines(row, width):
    sin_d, cos_d = sincos_turns(row * (LANES / width))
    rows = row.shape[1]
    return columns_of(sin_d, rows), columns_of(cos_d, rows)


def sine_start(row, term0, width):
    sin_d, cos_d = step_sines(row, width)
    focus = columns_of(row, row.shape[1])
    sin0, cos0 = sincos_turns(focus * ((term0 + 1.0) / width) + 0.1 / (2.0 * math.pi))
    return sin0, sin0 * cos_d - cos0 * sin_d, 2.0 * cos_d


def wait_bytes(ref, sem):
    pltpu.make_async_copy(ref, ref, sem).wait()


def score_kernel(n_img, n_proj, x_size, img_hbm, proj_hbm, noise_hbm, focus_hbm, count_hbm, limit_hbm, plan_hbm,
                 posts_ref, back_img, back_wgt, ev_ref,
                 img, proj, noise_ref, focus_ref, count_ref, limit_ref, plan_ref, weighted, weighted_sq, total,
                 sine, moved, contrast, focus_all, limit_all, terms, every_terms, stats, every_stats,
                 load_sem, img_load, proj_load, up_token, down_token,
                 small_send, small_recv, near_sem, img_send, img_recv, pass_send, pass_recv,
                 post_send, post_recv, stat_send, stat_recv):
    me = lax.axis_index("img")
    mine = lax.axis_index("proj")
    img_rows, width = img.shape
    proj_rows = proj.shape[0]
    part = width // n_img
    chips = n_img // 2
    z_size = n_proj // x_size
    row_y, core = me // 2, lax.rem(me, 2)
    at_x, at_z = lax.rem(mine, x_size), mine // x_size
    bottom, top = at_z == 0, at_z == z_size - 1

    def img_to(t):
        return lax.rem(row_y + t // 2, chips) * 2 + lax.rem(core + lax.rem(t, 2), 2)

    def img_from(t):
        return lax.rem(row_y + chips - t // 2, chips) * 2 + lax.rem(core + t % 2, 2)

    side = lax.rem(at_x + at_z, 2)
    across = (mine + 1 - 2 * lax.rem(at_x, 2), mine + x_size * (1 - 2 * lax.rem(at_z, 2)))
    piece = img_rows // 2 // PIECES

    def signal(sem, img, proj):
        pl.semaphore_signal(sem, inc=1, device_id={"img": img, "proj": proj}, device_id_type=MESH)

    barrier = pltpu.get_barrier_semaphore()
    for k in range(x_size):
        for t in range(n_img):
            if k or t:
                signal(barrier, img_to(t), at_z * x_size + lax.rem(at_x + k, x_size))
    pl.when(jnp.logical_not(top))(lambda: signal(barrier, me, mine + x_size))
    pl.when(jnp.logical_not(bottom))(lambda: signal(barrier, me, mine - x_size))

    small_loads = [pltpu.make_async_copy(source, target, load_sem.at[n]) for n, (source, target) in enumerate(
        ((focus_hbm, focus_ref), (limit_hbm, limit_ref), (noise_hbm, noise_ref), (count_hbm, count_ref),
         (plan_hbm, plan_ref)))]
    wide = 2 * DEPTH
    steps = width // wide

    def load_img(n):
        cols = pl.ds(pl.multiple_of(n * wide, wide), wide)
        return pltpu.make_async_copy(img_hbm.at[:, cols], img.at[:, cols], img_load.at[n])

    def load_proj(n):
        cols = pl.ds(pl.multiple_of(n * wide, wide), wide)
        return pltpu.make_async_copy(proj_hbm.at[:, cols], proj.at[:, cols], proj_load.at[n])

    for load in small_loads[:3]:
        load.start()
    load_img(0).start()
    for n in range(steps):
        load_proj(n).start()
        if n + 1 < steps:
            load_img(n + 1).start()
    for load in small_loads[3:]:
        load.start()
    with jax.named_scope("small"):
        small_loads[0].wait()
        small_loads[1].wait()

    lane = lax.broadcasted_iota(jnp.int32, (1, LANES), 1).astype(jnp.float32)
    sine[0], sine[1], sine[2] = sine_start(focus_ref[...], lane, width)
    sine[3] = columns_of(limit_ref[...].astype(jnp.float32), img_rows)
    total[...] = jnp.zeros_like(total)
    small_loads[2].wait()
    contract = (((1,), (1,)), ((), ()))
    strip = 16

    def terms_chunk(c, slot):
        starts = [pl.multiple_of(c * DEPTH + k * LANES, LANES) for k in range(DEPTH // LANES)]
        noise = [noise_ref[:, pl.ds(start, LANES)] for start in starts]
        term = [lane + start.astype(jnp.float32) for start in starts]
        for r in range(img_rows // strip):
            rows = slice(r * strip, (r + 1) * strip)
            sin_v, sin_before, turn, limit = sine[0, rows], sine[1, rows], sine[2, rows], sine[3, rows]
            for k, start in enumerate(starts):
                cols = slice(k * LANES, (k + 1) * LANES)
                noisy = jnp.where(term[k] < limit, sin_v, 0.0) * noise[k]
                pixels = img[rows, pl.ds(start, LANES)].astype(jnp.float32)
                weighted[slot, rows, cols] = (noisy * pixels).astype(jnp.bfloat16)
                weighted_sq[slot, rows, cols] = (noisy * (-0.5 * sin_v)).astype(jnp.bfloat16)
                sin_v, sin_before = turn * sin_v - sin_before, sin_v
            sine[0, rows] = sin_v
            sine[1, rows] = sin_before

    def score_chunk(c, slot):
        rows = proj[:, pl.ds(pl.multiple_of(c * DEPTH, DEPTH), DEPTH)]
        got = lax.dot_general(rows, weighted[slot], contract, preferred_element_type=jnp.float32)
        got = got + lax.dot_general(rows * rows, weighted_sq[slot], contract, preferred_element_type=jnp.float32)
        total[...] += got

    def move_img(t, n):
        rows = pl.ds(pl.multiple_of((side * PIECES + n) * piece, piece), piece)
        slab = pl.ds(pl.multiple_of(img_to(t) * part, LANES), part)
        return pltpu.make_async_remote_copy(
            src_ref=img_hbm.at[rows, slab], dst_ref=moved.at[t, rows, :], send_sem=img_send,
            recv_sem=img_recv.at[t - 2, n], device_id={"img": img_to(t)}, device_id_type=MESH)

    near = pltpu.make_async_remote_copy(
        src_ref=img_hbm.at[:, pl.ds(pl.multiple_of(img_to(1) * part, LANES), part)], dst_ref=moved.at[1],
        send_sem=near_sem.at[0], recv_sem=near_sem.at[1], device_id={"img": img_to(1)}, device_id_type=MESH)
    small = [pltpu.make_async_remote_copy(
        src_ref=ref, dst_ref=dst.at[t], send_sem=small_send.at[n], recv_sem=small_recv.at[n],
        device_id={"img": img_to(t)}, device_id_type=MESH)
        for t in range(1, n_img) for n, (ref, dst) in enumerate(((focus_ref, focus_all), (limit_ref, limit_all)))]
    far = [(t, n) for n in range(PIECES) for t in range(2, n_img)]

    with jax.named_scope("img0"):
        load_img(0).wait()
    terms_chunk(jnp.int32(0), 0)

    def score_step(i, carry):
        with jax.named_scope("loads"):
            load_proj(i).wait()
            pl.when(i + 1 < steps)(lambda: load_img(i + 1).wait())

        @pl.when(i == NEAR_STEP)
        def _():
            with jax.named_scope("near"):
                pl.semaphore_wait(barrier, n_img * x_size - 1 + jnp.where(bottom, 0, 1) + jnp.where(top, 0, 1))
            pl.when(bottom)(lambda: signal(up_token, me, mine + x_size))
            pl.when(top)(lambda: signal(down_token, me, mine - x_size))
            for copy in small:
                copy.start()
            for t, n in far:
                move_img(t, n).start()
            near.start()

        score_chunk(2 * i, 0)
        terms_chunk(2 * i + 1, 1)
        score_chunk(2 * i + 1, 1)
        terms_chunk(jnp.minimum(2 * i + 2, width // DEPTH - 1), 0)
        return carry

    lax.fori_loop(0, steps, score_step, 0)

    with jax.named_scope("smax"):
        small_loads[3].wait()
        small_loads[4].wait()
    scores = total[...]
    orient = lax.broadcasted_iota(jnp.int32, (proj_rows, img_rows), 0) + mine * proj_rows
    significant = orient < count_ref[...]
    masked = jnp.where(significant, scores, -1e30)
    peak = jnp.max(masked, axis=0, keepdims=True)
    expo = jnp.where(significant, jnp.exp(masked - peak), 0.0)
    stats[0:1, :] = peak
    stats[1:2, :] = jnp.sum(expo, axis=0, keepdims=True)
    terms[...] = expo.astype(jnp.bfloat16)

    def send_stat(k, carry):
        target, t = k // n_img, lax.rem(k, n_img)
        slot = t * n_proj + lax.rem(target - mine + n_proj, n_proj)

        @pl.when(slot > 0)
        def _():
            pltpu.make_async_remote_copy(
                src_ref=stats, dst_ref=every_stats.at[slot], send_sem=stat_send, recv_sem=stat_recv,
                device_id={"img": img_to(t), "proj": target}, device_id_type=MESH).start()
        return carry

    plane = x_size * n_img

    @pl.when(jnp.logical_not(bottom))
    def _():
        with jax.named_scope("up"):
            pl.semaphore_wait(up_token, 1)
        pl.when(jnp.logical_not(top))(lambda: signal(up_token, me, mine + x_size))

    with jax.named_scope("send"):
        lax.fori_loop(0, (at_z + 1) * plane, send_stat, 0)

    def learn_above():
        with jax.named_scope("down"):
            pl.semaphore_wait(down_token, 1)
        pl.when(jnp.logical_not(bottom))(lambda: signal(down_token, me, mine - x_size))
        lax.fori_loop((at_z + 1) * plane, z_size * plane, send_stat, 0)

    inner = jnp.logical_not(jnp.logical_or(bottom, top))
    pl.when(jnp.logical_and(inner, at_z == z_size - 2))(learn_above)

    post_copies = {t: pltpu.make_async_remote_copy(
        src_ref=terms, dst_ref=every_terms.at[t], send_sem=post_send, recv_sem=post_recv.at[t - 1],
        device_id={"img": img_to(t)}, device_id_type=MESH) for t in (1, *range(2, n_img, 2))}
    for t in range(2, n_img, 2):
        post_copies[t + 1] = pltpu.make_async_remote_copy(
            src_ref=every_terms.at[t], dst_ref=every_terms.at[t + 1], send_sem=post_send,
            recv_sem=post_recv.at[t], device_id={"img": img_to(1)}, device_id_type=MESH)
    for t in (*range(2, n_img, 2), 1):
        post_copies[t].start()

    term0 = lane + (me * part).astype(jnp.float32)

    def weights_block(t, carry):
        sine[0], sine[1], sine[2] = sine_start(focus_all[t], term0, width)
        sine[3] = columns_of(limit_all[t].astype(jnp.float32), img_rows)
        for r in range(img_rows // strip):
            inside = slice(r * strip, (r + 1) * strip)
            rows = pl.ds(pl.multiple_of(t * img_rows + r * strip, strip), strip)
            sin_v, sin_before, turn, limit = sine[0, inside], sine[1, inside], sine[2, inside], sine[3, inside]
            for c in range(part // LANES):
                cols = slice(c * LANES, (c + 1) * LANES)
                kept = jnp.where(term0 + float(c * LANES) < limit, sin_v, 0.0)
                contrast[rows, cols] = kept
                back_wgt[rows, cols] = (kept * sin_v).astype(jnp.bfloat16)
                sin_v, sin_before = turn * sin_v - sin_before, sin_v
        return carry

    def take_images(t, first, pixels):
        rows = pl.ds(pl.multiple_of(t * img_rows + first, piece), pixels.shape[0])
        back_img[rows, :] = (contrast[rows, :] * pixels.astype(jnp.float32)).astype(jnp.bfloat16)

    def take_piece(t, half, n):
        first = pl.multiple_of((half * PIECES + n) * piece, piece)
        take_images(t, first, moved[t, pl.ds(first, piece), :])

    passed = []

    def pass_on(t, n):
        with jax.named_scope(f"mv{t}{n}"):
            move_img(t, n).wait_recv()
        held = moved.at[t, pl.ds(pl.multiple_of((side * PIECES + n) * piece, piece), piece), :]
        passed.append(pltpu.make_async_remote_copy(
            src_ref=held, dst_ref=held, send_sem=pass_send, recv_sem=pass_recv.at[t - 2, n],
            device_id={"proj": across[n % 2]}, device_id_type=MESH))
        passed[-1].start()

    focus_all[0] = focus_ref[...]
    limit_all[0] = limit_ref[...]
    with jax.named_scope("smallx"):
        for n, every in enumerate((focus_all, limit_all)):
            wait_bytes(every.at[pl.ds(1, n_img - 1)], small_recv.at[n])
    per_piece = n_img - 2
    with jax.named_scope("weights"):
        lax.fori_loop(0, n_img // 2, weights_block, 0)
    for t, n in far[:per_piece]:
        pass_on(t, n)
    pl.when(jnp.logical_and(inner, at_z != z_size - 2))(learn_above)
    lax.fori_loop(n_img // 2, n_img, weights_block, 0)
    for t, n in far[per_piece:2 * per_piece]:
        pass_on(t, n)
    take_images(0, 0, img[:, pl.ds(pl.multiple_of(me * part, LANES), part)])
    with jax.named_scope("nearimg"):
        near.wait()
    take_images(1, 0, moved[1])
    pl.when(jnp.logical_and(bottom, jnp.logical_not(top)))(learn_above)
    for t, n in far[2 * per_piece:]:
        pass_on(t, n)
    for t in range(2, n_img, 2):
        with jax.named_scope(f"post{t}"):
            post_copies[t].wait_recv()
        post_copies[t + 1].start()
    for t, n in far:
        take_piece(t, side, n)

    every_stats[0] = stats[...]
    with jax.named_scope("stat"):
        wait_bytes(every_stats.at[pl.ds(1, n_img * n_proj - 1)], stat_recv)
    evidence = []
    for t in range(n_img):
        every = every_stats[pl.ds(t * n_proj, n_proj)]
        peaks, masses = every[:, 0, :], every[:, 1, :]
        highest = jnp.max(peaks, axis=0, keepdims=True)
        whole = jnp.sum(masses * jnp.exp(peaks - highest), axis=0, keepdims=True)
        evidence.append(highest + jnp.log(whole))
        scale = jnp.exp(peaks[0:1, :] - evidence[t])
        if t % 2:
            with jax.named_scope(f"post{t}"):
                post_copies[t].wait_recv()
        values = every_terms[t].astype(jnp.float32) if t else terms[...].astype(jnp.float32)
        posts_ref[:, t * img_rows:(t + 1) * img_rows] = (values * scale).astype(jnp.bfloat16)

    groups = img_rows // BLOCK
    group = lax.broadcasted_iota(jnp.int32, (1, img_rows), 1) // BLOCK
    placed = jnp.zeros((1, img_rows), jnp.float32)
    for t in range(n_img):
        plan = jnp.zeros((1, img_rows), jnp.int32)
        for g in range(groups):
            plan = jnp.where(group == g, plan_ref[img_from(t) * groups + g], plan)
        for s in range(groups):
            turned, target = evidence[t], plan
            if s:
                turned = pltpu.roll(evidence[t], s * BLOCK, 1)
                target = pltpu.roll(plan, s * BLOCK, 1)
            placed = placed + jnp.where(target == me * groups + group, turned, 0.0)
    ev_ref[...] = placed

    wait_bytes(every_stats.at[pl.ds(1, n_img * n_proj - 1)], stat_send)
    for n, every in enumerate((focus_all, limit_all)):
        wait_bytes(every.at[pl.ds(1, n_img - 1)], small_send.at[n])
    wait_bytes(every_terms.at[pl.ds(1, n_img - 1)], post_send)
    wait_bytes(moved.at[pl.ds(2, n_img - 2), pl.ds(0, img_rows // 2)], img_send)
    for q, (t, n) in enumerate(far):
        with jax.named_scope(f"ps{q}"):
            passed[q].wait_recv()
        take_piece(t, 1 - side, n)
    wait_bytes(moved.at[pl.ds(2, n_img - 2), pl.ds(0, img_rows // 2)], pass_send)


def back_kernel(posts_ref, back_img, back_wgt, ev_ref, rec_hbm, placed_hbm, rec, out_sem):
    part = back_img.shape[1]
    step = min(part, 256)
    steps = part // step
    posts = posts_ref[...]
    last = pltpu.make_async_copy(ev_ref, placed_hbm, out_sem.at[steps])
    last.start()
    copies = [last]
    for c in range(steps):
        cols = slice(c * step, (c + 1) * step)
        sums = jnp.dot(posts, back_img[:, cols], preferred_element_type=jnp.float32)
        weights = jnp.dot(posts, back_wgt[:, cols], preferred_element_type=jnp.float32)
        rec[:, cols] = (sums / (weights + 1.0)).astype(jnp.bfloat16)
        copies.append(pltpu.make_async_copy(rec.at[:, cols], rec_hbm.at[:, cols], out_sem.at[c]))
        copies[-1].start()
    for copy in copies:
        copy.wait()


def shards(n_img, n_proj, images, projections, noise_weight, defocus, orient_count, term_limit, block_plan):
    img_rows, width = images.shape
    proj_rows = projections.shape[0]
    part = width // n_img
    x_size = 1 << ((n_proj.bit_length() - 1) // 2)
    vmem = pl.BlockSpec(memory_space=pltpu.VMEM)
    hbm = pl.BlockSpec(memory_space=pl.ANY)
    bf16, f32, i32 = jnp.bfloat16, jnp.float32, jnp.int32
    dma, regular = pltpu.SemaphoreType.DMA, pltpu.SemaphoreType.REGULAR
    held = pl.pallas_call(
        functools.partial(score_kernel, n_img, n_proj, x_size),
        out_shape=(pltpu.VMEM((proj_rows, n_img * img_rows), bf16), pltpu.VMEM((n_img * img_rows, part), bf16),
                   pltpu.VMEM((n_img * img_rows, part), bf16), pltpu.VMEM((1, img_rows), f32)),
        in_specs=[hbm] * 7,
        out_specs=(vmem, vmem, vmem, vmem),
        scratch_shapes=[
            pltpu.VMEM((img_rows, width), bf16),
            pltpu.VMEM((proj_rows, width), bf16),
            pltpu.VMEM((1, width), f32),
            pltpu.VMEM((1, img_rows), f32),
            pltpu.VMEM((1, img_rows), i32),
            pltpu.VMEM((1, img_rows), i32),
            pltpu.SMEM(block_plan.shape, i32),
            pltpu.VMEM((2, img_rows, DEPTH), bf16),
            pltpu.VMEM((2, img_rows, DEPTH), bf16),
            pltpu.VMEM((proj_rows, img_rows), f32),
            pltpu.VMEM((4, img_rows, LANES), f32),
            pltpu.VMEM((n_img, img_rows, part), bf16),
            pltpu.VMEM((n_img * img_rows, part), f32),
            pltpu.VMEM((n_img, 1, img_rows), f32),
            pltpu.VMEM((n_img, 1, img_rows), i32),
            pltpu.VMEM((proj_rows, img_rows), bf16),
            pltpu.VMEM((n_img, proj_rows, img_rows), bf16),
            pltpu.VMEM((2, img_rows), f32),
            pltpu.VMEM((n_img * n_proj, 2, img_rows), f32),
            dma((5,)), dma((width // DEPTH // 2,)), dma((width // DEPTH // 2,)), regular, regular,
            dma((2,)), dma((2,)), dma((2,)), dma, dma((n_img - 2, PIECES)), dma, dma((n_img - 2, PIECES)),
            dma, dma((n_img - 1,)), dma, dma,
        ],
        compiler_params=pltpu.CompilerParams(
            collective_id=0, has_side_effects=True, vmem_limit_bytes=54 * 1024 * 1024),
    )(images, projections, noise_weight.reshape(1, -1), defocus.reshape(1, -1), orient_count.reshape(1, -1),
      term_limit.reshape(1, -1), block_plan)
    reconstruction, evidence = pl.pallas_call(
        back_kernel,
        out_shape=(jax.ShapeDtypeStruct((proj_rows, part), bf16), jax.ShapeDtypeStruct((1, img_rows), f32)),
        in_specs=[vmem] * 4,
        out_specs=(hbm, hbm),
        scratch_shapes=[pltpu.VMEM((proj_rows, part), bf16), dma((part // min(part, 256) + 1,))],
        compiler_params=pltpu.CompilerParams(vmem_limit_bytes=16 * 1024 * 1024),
    )(*held)
    return reconstruction, evidence.reshape(-1)


def solution(mesh):
    n_img, n_proj = mesh.shape["img"], mesh.shape["proj"]
    placed = (P("img", None), P("proj", None), P(), P("img"), P("img"), P("img"), P())
    return jax.shard_map(
        functools.partial(shards, n_img, n_proj), mesh=mesh, in_specs=placed,
        out_specs=(P("proj", "img"), P("img")), check_vma=False,
    )
```

time: 23 us -> 19 us (0.83)
  Pallas kernels: 22.2 us -> 18.2 us
    pallas_call x1, Pallas kernels: 20.6 us -> 16.7 us  [shards(): pl.pallas_call(functools.partial(score_kernel, n_img, n_proj, x_size), ou...]
where the time goes in v2:
time: 19 us; the launch traced here: 18.9 us
  Pallas kernels  18.2 us (96%)
  between operations  0.64 us (3%)
    pallas_call x1, Pallas kernels, shards(): pl.pallas_call(functools.partial(score_kernel, n_img, n_proj, x_size), ou...  16.7 us
    pallas_call x1, Pallas kernels, shards(): pl.pallas_call(back_kernel, out_shape=(jax.ShapeDtypeStruct((proj_rows, p...  1.58 us

profile of v2, /device:TPU:0, one launch (start us, length us, event | category | flops | bytes accessed | tf_op | source)
XLA Modules:
  0.0 18.9 jit_solution(13046711533100970065)
XLA Ops:
  0.6 16.7 %shard_map.86 = (bf16[320,512]{1,0:T(8,128)(2,1)S(1)}, bf16[512,1024]{1,0:T(8,128)(2,1)S(1)}, bf16[512,1024]{1,0:T(8,128)(2,1)S(1)}, f32[1,128]{1,0:T(1,128)S(1)}) custom-call(bf16[128,4096]{1,0:T(8,128)(2,1)} %img_hbm.1, bf16[320,4096]{1,0:T(8,128)(2,1)} %proj_hbm.1, f32[1,4096]{1,0:T(1,128)} %bitcast.5, f32[1,128]{1,0:T(1,128)} %bitcast.6, ...), custom_call_target="tpu_custom_call" | custom-call | tf_op jit(solution)/shard_map/pallas_call | solution.py:389
  17.3 1.6 %shard_map.87 = (bf16[320,1024]{1,0:T(8,128)(2,1)}, f32[1,128]{1,0:T(1,128)}) custom-call(bf16[320,512]{1,0:T(8,128)(2,1)S(1)} %get-tuple-element.8.posts_ref, bf16[512,1024]{1,0:T(8,128)(2,1)S(1)} %get-tuple-element.9.back_img, bf16[512,1024]{1,0:T(8,128)(2,1)S(1)} %get-tuple-element.10.back_wgt, f32[1,128]{1,0:T(1,128)S(1)} %get-tuple-element.11.ev_ref), custom_call_target="tpu_custom_call" | custom-call | tf_op jit(solution)/shard_map/pallas_call | solution.py:423

commit v3 on v2

--- a/solution.py
+++ b/solution.py
@@ -9,7 +9,8 @@
 from jax.sharding import PartitionSpec as P
 
 BLOCK = 32
-PIECES = 4
+PIECES = 2
+PIECE = 16
 LANES = 128
 DEPTH = 512
 NEAR_STEP = 1
@@ -58,7 +59,7 @@
                  posts_ref, back_img, back_wgt, ev_ref,
                  img, proj, noise_ref, focus_ref, count_ref, limit_ref, plan_ref, weighted, weighted_sq, total,
                  sine, moved, contrast, focus_all, limit_all, terms, every_terms, stats, every_stats,
-                 load_sem, img_load, proj_load, up_token, down_token,
+                 load_sem, img_load, proj_load, next_token, all_token,
                  small_send, small_recv, near_sem, img_send, img_recv, pass_send, pass_recv,
                  post_send, post_recv, stat_send, stat_recv):
     me = lax.axis_index("img")
@@ -67,10 +68,8 @@
     proj_rows = proj.shape[0]
     part = width // n_img
     chips = n_img // 2
-    z_size = n_proj // x_size
     row_y, core = me // 2, lax.rem(me, 2)
     at_x, at_z = lax.rem(mine, x_size), mine // x_size
-    bottom, top = at_z == 0, at_z == z_size - 1
 
     def img_to(t):
         return lax.rem(row_y + t // 2, chips) * 2 + lax.rem(core + lax.rem(t, 2), 2)
@@ -78,20 +77,54 @@
     def img_from(t):
         return lax.rem(row_y + chips - t // 2, chips) * 2 + lax.rem(core + t % 2, 2)
 
-    side = lax.rem(at_x + at_z, 2)
-    across = (mine + 1 - 2 * lax.rem(at_x, 2), mine + x_size * (1 - 2 * lax.rem(at_z, 2)))
-    piece = img_rows // 2 // PIECES
+    odd_x, odd_z = lax.rem(at_x, 2), lax.rem(at_z, 2)
+    side = lax.rem(odd_x + odd_z, 2)
+    beside_x, beside_z = mine + 1 - 2 * odd_x, mine + x_size * (1 - 2 * odd_z)
+    beside_xz = beside_x + beside_z - mine
+    quarter = (img_rows - 2 * PIECES * PIECE) // 4
+
+    def half_rows(k, n):
+        return pl.ds(pl.multiple_of((k * PIECES + n) * PIECE, PIECE), PIECE)
+
+    def quarter_rows(x, z):
+        return pl.ds(pl.multiple_of(2 * PIECES * PIECE + (x * 2 + z) * quarter, 8), quarter)
 
     def signal(sem, img, proj):
         pl.semaphore_signal(sem, inc=1, device_id={"img": img, "proj": proj}, device_id_type=MESH)
 
     barrier = pltpu.get_barrier_semaphore()
-    for k in range(x_size):
-        for t in range(n_img):
-            if k or t:
-                signal(barrier, img_to(t), at_z * x_size + lax.rem(at_x + k, x_size))
-    pl.when(jnp.logical_not(top))(lambda: signal(barrier, me, mine + x_size))
-    pl.when(jnp.logical_not(bottom))(lambda: signal(barrier, me, mine - x_size))
+    partner, first_core = img_to(1), core == 0
+
+    def greet_next(t, proj):
+        signal(barrier, img_to(t) - lax.rem(img_to(t), 2), proj)
+
+    for k in range(1, x_size):
+        greet_next(0, at_z * x_size + lax.rem(at_x + k, x_size))
+    for t in range(2, n_img, 2):
+        greet_next(t, mine)
+    pl.when(jnp.logical_not(first_core))(lambda: signal(barrier, partner, mine))
+
+    def greet_all(k, carry):
+        chip, proj = k // n_proj, lax.rem(k, n_proj)
+        row = chip * 2 + 1
+        pl.when(jnp.logical_or(row != me, proj != mine))(lambda: signal(barrier, row, proj))
+        return carry
+
+    def meet_next():
+        with jax.named_scope("near"):
+            @pl.when(first_core)
+            def _():
+                pl.semaphore_wait(barrier, 2 * (chips - 1) + 2 * (x_size - 1) + 1)
+                signal(next_token, partner, mine)
+            pl.when(jnp.logical_not(first_core))(lambda: pl.semaphore_wait(next_token, 1))
+
+    def meet_all():
+        with jax.named_scope("all"):
+            @pl.when(jnp.logical_not(first_core))
+            def _():
+                pl.semaphore_wait(barrier, n_img * n_proj - 1)
+                signal(all_token, partner, mine)
+            pl.when(first_core)(lambda: pl.semaphore_wait(all_token, 1))
 
     small_loads = [pltpu.make_async_copy(source, target, load_sem.at[n]) for n, (source, target) in enumerate(
         ((focus_hbm, focus_ref), (limit_hbm, limit_ref), (noise_hbm, noise_ref), (count_hbm, count_ref),
@@ -116,6 +149,7 @@
             load_img(n + 1).start()
     for load in small_loads[3:]:
         load.start()
+    lax.fori_loop(0, chips * n_proj, greet_all, 0)
     with jax.named_scope("small"):
         small_loads[0].wait()
         small_loads[1].wait()
@@ -151,12 +185,19 @@
         got = got + lax.dot_general(rows * rows, weighted_sq[slot], contract, preferred_element_type=jnp.float32)
         total[...] += got
 
+    my_rows = [quarter_rows(odd_x, odd_z)] + [half_rows(side, n) for n in range(PIECES)]
+
     def move_img(t, n):
-        rows = pl.ds(pl.multiple_of((side * PIECES + n) * piece, piece), piece)
         slab = pl.ds(pl.multiple_of(img_to(t) * part, LANES), part)
         return pltpu.make_async_remote_copy(
-            src_ref=img_hbm.at[rows, slab], dst_ref=moved.at[t, rows, :], send_sem=img_send,
+            src_ref=img_hbm.at[my_rows[n], slab], dst_ref=moved.at[t, my_rows[n], :], send_sem=img_send,
             recv_sem=img_recv.at[t - 2, n], device_id={"img": img_to(t)}, device_id_type=MESH)
+
+    def pass_rows(t, rows, proj):
+        held = moved.at[t, rows, :]
+        pltpu.make_async_remote_copy(
+            src_ref=held, dst_ref=held, send_sem=pass_send, recv_sem=pass_recv, device_id={"proj": proj},
+            device_id_type=MESH).start()
 
     near = pltpu.make_async_remote_copy(
         src_ref=img_hbm.at[:, pl.ds(pl.multiple_of(img_to(1) * part, LANES), part)], dst_ref=moved.at[1],
@@ -165,7 +206,7 @@
         src_ref=ref, dst_ref=dst.at[t], send_sem=small_send.at[n], recv_sem=small_recv.at[n],
         device_id={"img": img_to(t)}, device_id_type=MESH)
         for t in range(1, n_img) for n, (ref, dst) in enumerate(((focus_ref, focus_all), (limit_ref, limit_all)))]
-    far = [(t, n) for n in range(PIECES) for t in range(2, n_img)]
+    far = [(t, n) for n in range(PIECES + 1) for t in range(2, n_img)]
 
     with jax.named_scope("img0"):
         load_img(0).wait()
@@ -178,10 +219,7 @@
 
         @pl.when(i == NEAR_STEP)
         def _():
-            with jax.named_scope("near"):
-                pl.semaphore_wait(barrier, n_img * x_size - 1 + jnp.where(bottom, 0, 1) + jnp.where(top, 0, 1))
-            pl.when(bottom)(lambda: signal(up_token, me, mine + x_size))
-            pl.when(top)(lambda: signal(down_token, me, mine - x_size))
+            meet_next()
             for copy in small:
                 copy.start()
             for t, n in far:
@@ -220,25 +258,9 @@
                 device_id={"img": img_to(t), "proj": target}, device_id_type=MESH).start()
         return carry
 
-    plane = x_size * n_img
-
-    @pl.when(jnp.logical_not(bottom))
-    def _():
-        with jax.named_scope("up"):
-            pl.semaphore_wait(up_token, 1)
-        pl.when(jnp.logical_not(top))(lambda: signal(up_token, me, mine + x_size))
-
+    meet_all()
     with jax.named_scope("send"):
-        lax.fori_loop(0, (at_z + 1) * plane, send_stat, 0)
-
-    def learn_above():
-        with jax.named_scope("down"):
-            pl.semaphore_wait(down_token, 1)
-        pl.when(jnp.logical_not(bottom))(lambda: signal(down_token, me, mine - x_size))
-        lax.fori_loop((at_z + 1) * plane, z_size * plane, send_stat, 0)
-
-    inner = jnp.logical_not(jnp.logical_or(bottom, top))
-    pl.when(jnp.logical_and(inner, at_z == z_size - 2))(learn_above)
+        lax.fori_loop(0, n_img * n_proj, send_stat, 0)
 
     post_copies = {t: pltpu.make_async_remote_copy(
         src_ref=terms, dst_ref=every_terms.at[t], send_sem=post_send, recv_sem=post_recv.at[t - 1],
@@ -247,8 +269,7 @@
         post_copies[t + 1] = pltpu.make_async_remote_copy(
             src_ref=every_terms.at[t], dst_ref=every_terms.at[t + 1], send_sem=post_send,
             recv_sem=post_recv.at[t], device_id={"img": img_to(1)}, device_id_type=MESH)
-    for t in (*range(2, n_img, 2), 1):
-        post_copies[t].start()
+    post_copies[1].start()
 
     term0 = lane + (me * part).astype(jnp.float32)
 
@@ -268,43 +289,45 @@
         return carry
 
     def take_images(t, first, pixels):
-        rows = pl.ds(pl.multiple_of(t * img_rows + first, piece), pixels.shape[0])
+        rows = pl.ds(pl.multiple_of(t * img_rows + first, 8), pixels.shape[0])
         back_img[rows, :] = (contrast[rows, :] * pixels.astype(jnp.float32)).astype(jnp.bfloat16)
 
-    def take_piece(t, half, n):
-        first = pl.multiple_of((half * PIECES + n) * piece, piece)
-        take_images(t, first, moved[t, pl.ds(first, piece), :])
-
-    passed = []
+    def take_rows(t, rows):
+        take_images(t, rows.start, moved[t, rows, :])
 
     def pass_on(t, n):
         with jax.named_scope(f"mv{t}{n}"):
             move_img(t, n).wait_recv()
-        held = moved.at[t, pl.ds(pl.multiple_of((side * PIECES + n) * piece, piece), piece), :]
-        passed.append(pltpu.make_async_remote_copy(
-            src_ref=held, dst_ref=held, send_sem=pass_send, recv_sem=pass_recv.at[t - 2, n],
-            device_id={"proj": across[n % 2]}, device_id_type=MESH))
-        passed[-1].start()
+        if n:
+            pass_rows(t, my_rows[n], (beside_x, beside_z)[(n + t) % 2])
+        else:
+            for proj in (beside_xz, beside_x, beside_z):
+                pass_rows(t, my_rows[0], proj)
+
+    other_rows = [quarter_rows(1 - odd_x, odd_z), quarter_rows(odd_x, 1 - odd_z), quarter_rows(1 - odd_x, 1 - odd_z)]
+    other_rows += [half_rows(1 - side, n) for n in range(PIECES)]
 
     focus_all[0] = focus_ref[...]
     limit_all[0] = limit_ref[...]
+    fill_weights = lambda lo, hi: lax.fori_loop(lo, hi, weights_block, 0)
+    fill_weights(0, 1)
     with jax.named_scope("smallx"):
         for n, every in enumerate((focus_all, limit_all)):
             wait_bytes(every.at[pl.ds(1, n_img - 1)], small_recv.at[n])
     per_piece = n_img - 2
-    with jax.named_scope("weights"):
-        lax.fori_loop(0, n_img // 2, weights_block, 0)
+    fill_weights(1, 2)
     for t, n in far[:per_piece]:
         pass_on(t, n)
-    pl.when(jnp.logical_and(inner, at_z != z_size - 2))(learn_above)
-    lax.fori_loop(n_img // 2, n_img, weights_block, 0)
+    fill_weights(2, 2 + per_piece // 2)
     for t, n in far[per_piece:2 * per_piece]:
         pass_on(t, n)
+    for t in range(2, n_img, 2):
+        post_copies[t].start()
+    fill_weights(2 + per_piece // 2, n_img)
     take_images(0, 0, img[:, pl.ds(pl.multiple_of(me * part, LANES), part)])
     with jax.named_scope("nearimg"):
         near.wait()
     take_images(1, 0, moved[1])
-    pl.when(jnp.logical_and(bottom, jnp.logical_not(top)))(learn_above)
     for t, n in far[2 * per_piece:]:
         pass_on(t, n)
     for t in range(2, n_img, 2):
@@ -312,7 +335,7 @@
             post_copies[t].wait_recv()
         post_copies[t + 1].start()
     for t, n in far:
-        take_piece(t, side, n)
+        take_rows(t, my_rows[n])
 
     every_stats[0] = stats[...]
     with jax.named_scope("stat"):
@@ -350,12 +373,15 @@
     for n, every in enumerate((focus_all, limit_all)):
         wait_bytes(every.at[pl.ds(1, n_img - 1)], small_send.at[n])
     wait_bytes(every_terms.at[pl.ds(1, n_img - 1)], post_send)
-    wait_bytes(moved.at[pl.ds(2, n_img - 2), pl.ds(0, img_rows // 2)], img_send)
-    for q, (t, n) in enumerate(far):
-        with jax.named_scope(f"ps{q}"):
-            passed[q].wait_recv()
-        take_piece(t, 1 - side, n)
-    wait_bytes(moved.at[pl.ds(2, n_img - 2), pl.ds(0, img_rows // 2)], pass_send)
+    sent, handed = PIECES * PIECE + quarter, PIECES * PIECE + 3 * quarter
+    wait_bytes(moved.at[pl.ds(2, n_img - 2), pl.ds(0, sent)], img_send)
+    handed_rows = moved.at[pl.ds(2, n_img - 2), pl.ds(0, handed)]
+    with jax.named_scope("pass"):
+        wait_bytes(handed_rows, pass_recv)
+    for t in range(2, n_img):
+        for rows in other_rows:
+            take_rows(t, rows)
+    wait_bytes(handed_rows, pass_send)
 
 
 def back_kernel(posts_ref, back_img, back_wgt, ev_ref, rec_hbm, placed_hbm, rec, out_sem):
@@ -413,7 +439,7 @@
             pltpu.VMEM((2, img_rows), f32),
             pltpu.VMEM((n_img * n_proj, 2, img_rows), f32),
             dma((5,)), dma((width // DEPTH // 2,)), dma((width // DEPTH // 2,)), regular, regular,
-            dma((2,)), dma((2,)), dma((2,)), dma, dma((n_img - 2, PIECES)), dma, dma((n_img - 2, PIECES)),
+            dma((2,)), dma((2,)), dma((2,)), dma, dma((n_img - 2, PIECES + 1)), dma, dma,
             dma, dma((n_img - 1,)), dma, dma,
         ],
         compiler_params=pltpu.CompilerParams(

time: 19 us -> 17.4 us (0.916)
  Pallas kernels: 18.2 us -> 16.6 us
    pallas_call x1, Pallas kernels: 16.7 us -> 15 us  [shards(): pl.pallas_call(functools.partial(score_kernel, n_img, n_proj, x_size), ou...]
where the time goes in v3:
time: 17.4 us; the launch traced here: 17.2 us
  Pallas kernels  16.6 us (95%)
  between operations  0.64 us (4%)
    pallas_call x1, Pallas kernels, shards(): pl.pallas_call(functools.partial(score_kernel, n_img, n_proj, x_size), ou...  15 us
    pallas_call x1, Pallas kernels, shards(): pl.pallas_call(back_kernel, out_shape=(jax.ShapeDtypeStruct((proj_rows, p...  1.58 us

profile of v3, /device:TPU:0, one launch (start us, length us, event | category | flops | bytes accessed | tf_op | source)
XLA Modules:
  0.0 17.2 jit_solution(13737229386478052835)
XLA Ops:
  0.6 15.0 %shard_map.86 = (bf16[320,512]{1,0:T(8,128)(2,1)S(1)}, bf16[512,1024]{1,0:T(8,128)(2,1)S(1)}, bf16[512,1024]{1,0:T(8,128)(2,1)S(1)}, f32[1,128]{1,0:T(1,128)S(1)}) custom-call(bf16[128,4096]{1,0:T(8,128)(2,1)} %img_hbm.1, bf16[320,4096]{1,0:T(8,128)(2,1)} %proj_hbm.1, f32[1,4096]{1,0:T(1,128)} %bitcast.5, f32[1,128]{1,0:T(1,128)} %bitcast.6, ...), custom_call_target="tpu_custom_call" | custom-call | tf_op jit(solution)/shard_map/pallas_call | solution.py:415
  15.7 1.6 %shard_map.87 = (bf16[320,1024]{1,0:T(8,128)(2,1)}, f32[1,128]{1,0:T(1,128)}) custom-call(bf16[320,512]{1,0:T(8,128)(2,1)S(1)} %get-tuple-element.8.posts_ref, bf16[512,1024]{1,0:T(8,128)(2,1)S(1)} %get-tuple-element.9.back_img, bf16[512,1024]{1,0:T(8,128)(2,1)S(1)} %get-tuple-element.10.back_wgt, f32[1,128]{1,0:T(1,128)S(1)} %get-tuple-element.11.ev_ref), custom_call_target="tpu_custom_call" | custom-call | tf_op jit(solution)/shard_map/pallas_call | solution.py:449

commit v4 on v3

--- a/solution.py
+++ b/solution.py
@@ -13,7 +13,6 @@
 PIECE = 16
 LANES = 128
 DEPTH = 512
-NEAR_STEP = 1
 MESH = pl.DeviceIdType.MESH
 SIN_TERMS = [(-1.0) ** k * math.pi ** (2 * k + 1) / math.factorial(2 * k + 1) for k in range(7)]
 COS_TERMS = [(-1.0) ** k * math.pi ** (2 * k) / math.factorial(2 * k) for k in range(8)]
@@ -104,19 +103,10 @@
         greet_next(t, mine)
     pl.when(jnp.logical_not(first_core))(lambda: signal(barrier, partner, mine))
 
-    def greet_all(k, carry):
-        chip, proj = k // n_proj, lax.rem(k, n_proj)
-        row = chip * 2 + 1
-        pl.when(jnp.logical_or(row != me, proj != mine))(lambda: signal(barrier, row, proj))
+    def greet_all(proj, carry):
+        for chip in range(chips):
+            pl.when(jnp.logical_or(chip * 2 + 1 != me, proj != mine))(lambda: signal(barrier, chip * 2 + 1, proj))
         return carry
-
-    def meet_next():
-        with jax.named_scope("near"):
-            @pl.when(first_core)
-            def _():
-                pl.semaphore_wait(barrier, 2 * (chips - 1) + 2 * (x_size - 1) + 1)
-                signal(next_token, partner, mine)
-            pl.when(jnp.logical_not(first_core))(lambda: pl.semaphore_wait(next_token, 1))
 
     def meet_all():
         with jax.named_scope("all"):
@@ -149,7 +139,45 @@
             load_img(n + 1).start()
     for load in small_loads[3:]:
         load.start()
-    lax.fori_loop(0, chips * n_proj, greet_all, 0)
+    with jax.named_scope('greet'):
+        lax.fori_loop(0, n_proj, greet_all, 0)
+    my_rows = [quarter_rows(odd_x, odd_z)] + [half_rows(side, n) for n in range(PIECES)]
+
+    def move_img(t, n):
+        slab = pl.ds(pl.multiple_of(img_to(t) * part, LANES), part)
+        return pltpu.make_async_remote_copy(
+            src_ref=img_hbm.at[my_rows[n], slab], dst_ref=moved.at[t, my_rows[n], :], send_sem=img_send,
+            recv_sem=img_recv.at[t - 2, n], device_id={"img": img_to(t)}, device_id_type=MESH)
+
+    def pass_rows(t, rows, proj):
+        held = moved.at[t, rows, :]
+        pltpu.make_async_remote_copy(
+            src_ref=held, dst_ref=held, send_sem=pass_send, recv_sem=pass_recv, device_id={"proj": proj},
+            device_id_type=MESH).start()
+
+    near = pltpu.make_async_remote_copy(
+        src_ref=img_hbm.at[:, pl.ds(pl.multiple_of(img_to(1) * part, LANES), part)], dst_ref=moved.at[1],
+        send_sem=near_sem.at[0], recv_sem=near_sem.at[1], device_id={"img": img_to(1)}, device_id_type=MESH)
+    small = [pltpu.make_async_remote_copy(
+        src_ref=ref, dst_ref=dst.at[t], send_sem=small_send.at[n], recv_sem=small_recv.at[n],
+        device_id={"img": img_to(t)}, device_id_type=MESH)
+        for t in range(1, n_img) for n, (ref, dst) in enumerate(((focus_hbm, focus_all), (limit_hbm, limit_all)))]
+    far = [(t, n) for n in range(PIECES + 1) for t in range(2, n_img)]
+
+    def send_images():
+        for copy in small:
+            copy.start()
+        for t, n in far:
+            move_img(t, n).start()
+        near.start()
+
+    @pl.when(first_core)
+    def _():
+        with jax.named_scope("near"):
+            pl.semaphore_wait(barrier, 2 * (chips - 1) + 2 * (x_size - 1) + 1)
+        signal(next_token, partner, mine)
+        send_images()
+
     with jax.named_scope("small"):
         small_loads[0].wait()
         small_loads[1].wait()
@@ -185,29 +213,6 @@
         got = got + lax.dot_general(rows * rows, weighted_sq[slot], contract, preferred_element_type=jnp.float32)
         total[...] += got
 
-    my_rows = [quarter_rows(odd_x, odd_z)] + [half_rows(side, n) for n in range(PIECES)]
-
-    def move_img(t, n):
-        slab = pl.ds(pl.multiple_of(img_to(t) * part, LANES), part)
-        return pltpu.make_async_remote_copy(
-            src_ref=img_hbm.at[my_rows[n], slab], dst_ref=moved.at[t, my_rows[n], :], send_sem=img_send,
-            recv_sem=img_recv.at[t - 2, n], device_id={"img": img_to(t)}, device_id_type=MESH)
-
-    def pass_rows(t, rows, proj):
-        held = moved.at[t, rows, :]
-        pltpu.make_async_remote_copy(
-            src_ref=held, dst_ref=held, send_sem=pass_send, recv_sem=pass_recv, device_id={"proj": proj},
-            device_id_type=MESH).start()
-
-    near = pltpu.make_async_remote_copy(
-        src_ref=img_hbm.at[:, pl.ds(pl.multiple_of(img_to(1) * part, LANES), part)], dst_ref=moved.at[1],
-        send_sem=near_sem.at[0], recv_sem=near_sem.at[1], device_id={"img": img_to(1)}, device_id_type=MESH)
-    small = [pltpu.make_async_remote_copy(
-        src_ref=ref, dst_ref=dst.at[t], send_sem=small_send.at[n], recv_sem=small_recv.at[n],
-        device_id={"img": img_to(t)}, device_id_type=MESH)
-        for t in range(1, n_img) for n, (ref, dst) in enumerate(((focus_ref, focus_all), (limit_ref, limit_all)))]
-    far = [(t, n) for n in range(PIECES + 1) for t in range(2, n_img)]
-
     with jax.named_scope("img0"):
         load_img(0).wait()
     terms_chunk(jnp.int32(0), 0)
@@ -217,14 +222,11 @@
             load_proj(i).wait()
             pl.when(i + 1 < steps)(lambda: load_img(i + 1).wait())
 
-        @pl.when(i == NEAR_STEP)
+        @pl.when(jnp.logical_and(i == 0, jnp.logical_not(first_core)))
         def _():
-            meet_next()
-            for copy in small:
-                copy.start()
-            for t, n in far:
-                move_img(t, n).start()
-            near.start()
+            with jax.named_scope("near"):
+                pl.semaphore_wait(next_token, 1)
+            send_images()
 
         score_chunk(2 * i, 0)
         terms_chunk(2 * i + 1, 1)
@@ -247,20 +249,36 @@
     stats[1:2, :] = jnp.sum(expo, axis=0, keepdims=True)
     terms[...] = expo.astype(jnp.bfloat16)
 
-    def send_stat(k, carry):
-        target, t = k // n_img, lax.rem(k, n_img)
-        slot = t * n_proj + lax.rem(target - mine + n_proj, n_proj)
-
-        @pl.when(slot > 0)
-        def _():
-            pltpu.make_async_remote_copy(
-                src_ref=stats, dst_ref=every_stats.at[slot], send_sem=stat_send, recv_sem=stat_recv,
-                device_id={"img": img_to(t), "proj": target}, device_id_type=MESH).start()
+    rows_of = [img_to(t) for t in range(n_img)]
+
+    def send_stats(target, carry):
+        ahead = target - mine
+        ahead = jnp.where(ahead < 0, ahead + n_proj, ahead)
+        for t in range(n_img):
+            copy = pltpu.make_async_remote_copy(
+                src_ref=stats, dst_ref=every_stats.at[t * n_proj + ahead], send_sem=stat_send, recv_sem=stat_recv,
+                device_id={"img": rows_of[t], "proj": target}, device_id_type=MESH)
+            if t:
+                copy.start()
+            else:
+                pl.when(target != mine)(copy.start)
         return carry
+
+    def pass_on(t, n):
+        with jax.named_scope(f"mv{t}{n}"):
+            move_img(t, n).wait_recv()
+        if n:
+            pass_rows(t, my_rows[n], (beside_x, beside_z)[(n + t) % 2])
+        else:
+            for proj in (beside_xz, beside_x, beside_z):
+                pass_rows(t, my_rows[0], proj)
 
     meet_all()
     with jax.named_scope("send"):
-        lax.fori_loop(0, n_img * n_proj, send_stat, 0)
+        lax.fori_loop(0, n_proj, send_stats, 0)
+    per_piece = n_img - 2
+    for t, n in far[:per_piece]:
+        pass_on(t, n)
 
     post_copies = {t: pltpu.make_async_remote_copy(
         src_ref=terms, dst_ref=every_terms.at[t], send_sem=post_send, recv_sem=post_recv.at[t - 1],
@@ -270,6 +288,8 @@
             src_ref=every_terms.at[t], dst_ref=every_terms.at[t + 1], send_sem=post_send,
             recv_sem=post_recv.at[t], device_id={"img": img_to(1)}, device_id_type=MESH)
     post_copies[1].start()
+    for t in range(2, n_img, 2):
+        post_copies[t].start()
 
     term0 = lane + (me * part).astype(jnp.float32)
 
@@ -295,15 +315,6 @@
     def take_rows(t, rows):
         take_images(t, rows.start, moved[t, rows, :])
 
-    def pass_on(t, n):
-        with jax.named_scope(f"mv{t}{n}"):
-            move_img(t, n).wait_recv()
-        if n:
-            pass_rows(t, my_rows[n], (beside_x, beside_z)[(n + t) % 2])
-        else:
-            for proj in (beside_xz, beside_x, beside_z):
-                pass_rows(t, my_rows[0], proj)
-
     other_rows = [quarter_rows(1 - odd_x, odd_z), quarter_rows(odd_x, 1 - odd_z), quarter_rows(1 - odd_x, 1 - odd_z)]
     other_rows += [half_rows(1 - side, n) for n in range(PIECES)]
 
@@ -314,15 +325,10 @@
     with jax.named_scope("smallx"):
         for n, every in enumerate((focus_all, limit_all)):
             wait_bytes(every.at[pl.ds(1, n_img - 1)], small_recv.at[n])
-    per_piece = n_img - 2
     fill_weights(1, 2)
-    for t, n in far[:per_piece]:
-        pass_on(t, n)
     fill_weights(2, 2 + per_piece // 2)
     for t, n in far[per_piece:2 * per_piece]:
         pass_on(t, n)
-    for t in range(2, n_img, 2):
-        post_copies[t].start()
     fill_weights(2 + per_piece // 2, n_img)
     take_images(0, 0, img[:, pl.ds(pl.multiple_of(me * part, LANES), part)])
     with jax.named_scope("nearimg"):

time: 17.4 us -> 16.7 us (0.960)
  Pallas kernels: 16.6 us -> 15.9 us
    pallas_call x1, Pallas kernels: 15 us -> 14.4 us  [shards(): pl.pallas_call(functools.partial(score_kernel, n_img, n_proj, x_size), ou...]
where the time goes in v4:
time: 16.7 us; the launch traced here: 16.6 us
  Pallas kernels  15.9 us (95%)
  between operations  0.64 us (4%)
    pallas_call x1, Pallas kernels, shards(): pl.pallas_call(functools.partial(score_kernel, n_img, n_proj, x_size), ou...  14.4 us
    pallas_call x1, Pallas kernels, shards(): pl.pallas_call(back_kernel, out_shape=(jax.ShapeDtypeStruct((proj_rows, p...  1.58 us

profile of v4, /device:TPU:0, one launch (start us, length us, event | category | flops | bytes accessed | tf_op | source)
XLA Modules:
  0.0 16.6 jit_solution(5525875322829504305)
XLA Ops:
  0.6 14.4 %shard_map.86 = (bf16[320,512]{1,0:T(8,128)(2,1)S(1)}, bf16[512,1024]{1,0:T(8,128)(2,1)S(1)}, bf16[512,1024]{1,0:T(8,128)(2,1)S(1)}, f32[1,128]{1,0:T(1,128)S(1)}) custom-call(bf16[128,4096]{1,0:T(8,128)(2,1)} %img_hbm.1, bf16[320,4096]{1,0:T(8,128)(2,1)} %proj_hbm.1, f32[1,4096]{1,0:T(1,128)} %bitcast.5, f32[1,128]{1,0:T(1,128)} %bitcast.6, ...), custom_call_target="tpu_custom_call" | custom-call | tf_op jit(solution)/shard_map/pallas_call | solution.py:421
  15.0 1.6 %shard_map.87 = (bf16[320,1024]{1,0:T(8,128)(2,1)}, f32[1,128]{1,0:T(1,128)}) custom-call(bf16[320,512]{1,0:T(8,128)(2,1)S(1)} %get-tuple-element.8.posts_ref, bf16[512,1024]{1,0:T(8,128)(2,1)S(1)} %get-tuple-element.9.back_img, bf16[512,1024]{1,0:T(8,128)(2,1)S(1)} %get-tuple-element.10.back_wgt, f32[1,128]{1,0:T(1,128)S(1)} %get-tuple-element.11.ev_ref), custom_call_target="tpu_custom_call" | custom-call | tf_op jit(solution)/shard_map/pallas_call | solution.py:455

commit v5 on v4

--- a/solution.py
+++ b/solution.py
@@ -11,6 +11,7 @@
 BLOCK = 32
 PIECES = 2
 PIECE = 16
+STEP = 256
 LANES = 128
 DEPTH = 512
 MESH = pl.DeviceIdType.MESH
@@ -55,7 +56,7 @@
 
 
 def score_kernel(n_img, n_proj, x_size, img_hbm, proj_hbm, noise_hbm, focus_hbm, count_hbm, limit_hbm, plan_hbm,
-                 posts_ref, back_img, back_wgt, ev_ref,
+                 posts_ref, back_img, back_wgt, near_img, near_wgt, ev_ref,
                  img, proj, noise_ref, focus_ref, count_ref, limit_ref, plan_ref, weighted, weighted_sq, total,
                  sine, moved, contrast, focus_all, limit_all, terms, every_terms, stats, every_stats,
                  load_sem, img_load, proj_load, next_token, all_token,
@@ -97,8 +98,6 @@
     def greet_next(t, proj):
         signal(barrier, img_to(t) - lax.rem(img_to(t), 2), proj)
 
-    for k in range(1, x_size):
-        greet_next(0, at_z * x_size + lax.rem(at_x + k, x_size))
     for t in range(2, n_img, 2):
         greet_next(t, mine)
     pl.when(jnp.logical_not(first_core))(lambda: signal(barrier, partner, mine))
@@ -149,10 +148,10 @@
             src_ref=img_hbm.at[my_rows[n], slab], dst_ref=moved.at[t, my_rows[n], :], send_sem=img_send,
             recv_sem=img_recv.at[t - 2, n], device_id={"img": img_to(t)}, device_id_type=MESH)
 
-    def pass_rows(t, rows, proj):
+    def pass_rows(t, rows, proj, sem):
         held = moved.at[t, rows, :]
         pltpu.make_async_remote_copy(
-            src_ref=held, dst_ref=held, send_sem=pass_send, recv_sem=pass_recv, device_id={"proj": proj},
+            src_ref=held, dst_ref=held, send_sem=pass_send, recv_sem=sem, device_id={"proj": proj},
             device_id_type=MESH).start()
 
     near = pltpu.make_async_remote_copy(
@@ -174,7 +173,7 @@
     @pl.when(first_core)
     def _():
         with jax.named_scope("near"):
-            pl.semaphore_wait(barrier, 2 * (chips - 1) + 2 * (x_size - 1) + 1)
+            pl.semaphore_wait(barrier, 2 * (chips - 1) + 1)
         signal(next_token, partner, mine)
         send_images()
 
@@ -268,17 +267,14 @@
         with jax.named_scope(f"mv{t}{n}"):
             move_img(t, n).wait_recv()
         if n:
-            pass_rows(t, my_rows[n], (beside_x, beside_z)[(n + t) % 2])
+            pass_rows(t, my_rows[n], (beside_x, beside_z)[(n + t) % 2], pass_recv.at[1])
         else:
             for proj in (beside_xz, beside_x, beside_z):
-                pass_rows(t, my_rows[0], proj)
+                pass_rows(t, my_rows[0], proj, pass_recv.at[0])
 
     meet_all()
     with jax.named_scope("send"):
         lax.fori_loop(0, n_proj, send_stats, 0)
-    per_piece = n_img - 2
-    for t, n in far[:per_piece]:
-        pass_on(t, n)
 
     post_copies = {t: pltpu.make_async_remote_copy(
         src_ref=terms, dst_ref=every_terms.at[t], send_sem=post_send, recv_sem=post_recv.at[t - 1],
@@ -288,6 +284,10 @@
             src_ref=every_terms.at[t], dst_ref=every_terms.at[t + 1], send_sem=post_send,
             recv_sem=post_recv.at[t], device_id={"img": img_to(1)}, device_id_type=MESH)
     post_copies[1].start()
+
+    per_piece = n_img - 2
+    for t, n in far[:per_piece]:
+        pass_on(t, n)
     for t in range(2, n_img, 2):
         post_copies[t].start()
 
@@ -315,8 +315,8 @@
     def take_rows(t, rows):
         take_images(t, rows.start, moved[t, rows, :])
 
-    other_rows = [quarter_rows(1 - odd_x, odd_z), quarter_rows(odd_x, 1 - odd_z), quarter_rows(1 - odd_x, 1 - odd_z)]
-    other_rows += [half_rows(1 - side, n) for n in range(PIECES)]
+    quarter_others = [quarter_rows(1 - odd_x, odd_z), quarter_rows(odd_x, 1 - odd_z), quarter_rows(1 - odd_x, 1 - odd_z)]
+    half_others = [half_rows(1 - side, n) for n in range(PIECES)]
 
     focus_all[0] = focus_ref[...]
     limit_all[0] = limit_ref[...]
@@ -346,7 +346,7 @@
     every_stats[0] = stats[...]
     with jax.named_scope("stat"):
         wait_bytes(every_stats.at[pl.ds(1, n_img * n_proj - 1)], stat_recv)
-    evidence = []
+    evidence, scales = [], []
     for t in range(n_img):
         every = every_stats[pl.ds(t * n_proj, n_proj)]
         peaks, masses = every[:, 0, :], every[:, 1, :]
@@ -354,11 +354,27 @@
         whole = jnp.sum(masses * jnp.exp(peaks - highest), axis=0, keepdims=True)
         evidence.append(highest + jnp.log(whole))
         scale = jnp.exp(peaks[0:1, :] - evidence[t])
+        scales.append(scale)
+
+    def place_posts(t):
         if t % 2:
             with jax.named_scope(f"post{t}"):
                 post_copies[t].wait_recv()
         values = every_terms[t].astype(jnp.float32) if t else terms[...].astype(jnp.float32)
-        posts_ref[:, t * img_rows:(t + 1) * img_rows] = (values * scale).astype(jnp.bfloat16)
+        posts_ref[:, t * img_rows:(t + 1) * img_rows] = (values * scales[t]).astype(jnp.bfloat16)
+
+    for t in range(2):
+        place_posts(t)
+    near_cols = 2 * img_rows
+    for c in range(part // STEP):
+        cols = slice(c * STEP, (c + 1) * STEP)
+        near_img[:, cols] = jnp.dot(posts_ref[:, :near_cols], back_img[:near_cols, cols],
+                                    preferred_element_type=jnp.float32)
+        near_wgt[:, cols] = jnp.dot(posts_ref[:, :near_cols], back_wgt[:near_cols, cols],
+                                    preferred_element_type=jnp.float32)
+
+    for t in range(2, n_img):
+        place_posts(t)
 
     groups = img_rows // BLOCK
     group = lax.broadcasted_iota(jnp.int32, (1, img_rows), 1) // BLOCK
@@ -379,29 +395,34 @@
     for n, every in enumerate((focus_all, limit_all)):
         wait_bytes(every.at[pl.ds(1, n_img - 1)], small_send.at[n])
     wait_bytes(every_terms.at[pl.ds(1, n_img - 1)], post_send)
-    sent, handed = PIECES * PIECE + quarter, PIECES * PIECE + 3 * quarter
-    wait_bytes(moved.at[pl.ds(2, n_img - 2), pl.ds(0, sent)], img_send)
-    handed_rows = moved.at[pl.ds(2, n_img - 2), pl.ds(0, handed)]
-    with jax.named_scope("pass"):
-        wait_bytes(handed_rows, pass_recv)
+    def far_bytes(rows):
+        return moved.at[pl.ds(2, n_img - 2), pl.ds(0, rows)]
+
+    wait_bytes(far_bytes(PIECES * PIECE + quarter), img_send)
+    with jax.named_scope("quart"):
+        wait_bytes(moved.at[pl.ds(2, n_img - 2), pl.ds(0, 3 * quarter)], pass_recv.at[0])
     for t in range(2, n_img):
-        for rows in other_rows:
+        for rows in quarter_others:
             take_rows(t, rows)
-    wait_bytes(handed_rows, pass_send)
-
-
-def back_kernel(posts_ref, back_img, back_wgt, ev_ref, rec_hbm, placed_hbm, rec, out_sem):
+    with jax.named_scope("half"):
+        wait_bytes(far_bytes(PIECES * PIECE), pass_recv.at[1])
+    for t in range(2, n_img):
+        for rows in half_others:
+            take_rows(t, rows)
+    wait_bytes(far_bytes(PIECES * PIECE + 3 * quarter), pass_send)
+
+
+def back_kernel(near_cols, posts_ref, back_img, back_wgt, near_img, near_wgt, ev_ref, rec_hbm, placed_hbm, rec, out_sem):
     part = back_img.shape[1]
-    step = min(part, 256)
-    steps = part // step
-    posts = posts_ref[...]
+    steps = part // STEP
+    posts = posts_ref[:, near_cols:]
     last = pltpu.make_async_copy(ev_ref, placed_hbm, out_sem.at[steps])
     last.start()
     copies = [last]
     for c in range(steps):
-        cols = slice(c * step, (c + 1) * step)
-        sums = jnp.dot(posts, back_img[:, cols], preferred_element_type=jnp.float32)
-        weights = jnp.dot(posts, back_wgt[:, cols], preferred_element_type=jnp.float32)
+        cols = slice(c * STEP, (c + 1) * STEP)
+        sums = near_img[:, cols] + jnp.dot(posts, back_img[near_cols:, cols], preferred_element_type=jnp.float32)
+        weights = near_wgt[:, cols] + jnp.dot(posts, back_wgt[near_cols:, cols], preferred_element_type=jnp.float32)
         rec[:, cols] = (sums / (weights + 1.0)).astype(jnp.bfloat16)
         copies.append(pltpu.make_async_copy(rec.at[:, cols], rec_hbm.at[:, cols], out_sem.at[c]))
         copies[-1].start()
@@ -421,9 +442,10 @@
     held = pl.pallas_call(
         functools.partial(score_kernel, n_img, n_proj, x_size),
         out_shape=(pltpu.VMEM((proj_rows, n_img * img_rows), bf16), pltpu.VMEM((n_img * img_rows, part), bf16),
-                   pltpu.VMEM((n_img * img_rows, part), bf16), pltpu.VMEM((1, img_rows), f32)),
+                   pltpu.VMEM((n_img * img_rows, part), bf16), pltpu.VMEM((proj_rows, part), f32),
+                   pltpu.VMEM((proj_rows, part), f32), pltpu.VMEM((1, img_rows), f32)),
         in_specs=[hbm] * 7,
-        out_specs=(vmem, vmem, vmem, vmem),
+        out_specs=(vmem,) * 6,
         scratch_shapes=[
             pltpu.VMEM((img_rows, width), bf16),
             pltpu.VMEM((proj_rows, width), bf16),
@@ -445,7 +467,7 @@
             pltpu.VMEM((2, img_rows), f32),
             pltpu.VMEM((n_img * n_proj, 2, img_rows), f32),
             dma((5,)), dma((width // DEPTH // 2,)), dma((width // DEPTH // 2,)), regular, regular,
-            dma((2,)), dma((2,)), dma((2,)), dma, dma((n_img - 2, PIECES + 1)), dma, dma,
+            dma((2,)), dma((2,)), dma((2,)), dma, dma((n_img - 2, PIECES + 1)), dma, dma((2,)),
             dma, dma((n_img - 1,)), dma, dma,
         ],
         compiler_params=pltpu.CompilerParams(
@@ -453,11 +475,11 @@
     )(images, projections, noise_weight.reshape(1, -1), defocus.reshape(1, -1), orient_count.reshape(1, -1),
       term_limit.reshape(1, -1), block_plan)
     reconstruction, evidence = pl.pallas_call(
-        back_kernel,
+        functools.partial(back_kernel, 2 * img_rows),
         out_shape=(jax.ShapeDtypeStruct((proj_rows, part), bf16), jax.ShapeDtypeStruct((1, img_rows), f32)),
-        in_specs=[vmem] * 4,
+        in_specs=[vmem] * 6,
         out_specs=(hbm, hbm),
-        scratch_shapes=[pltpu.VMEM((proj_rows, part), bf16), dma((part // min(part, 256) + 1,))],
+        scratch_shapes=[pltpu.VMEM((proj_rows, part), bf16), dma((part // STEP + 1,))],
         compiler_params=pltpu.CompilerParams(vmem_limit_bytes=16 * 1024 * 1024),
     )(*held)
     return reconstruction, evidence.reshape(-1)

time: 16.7 us -> 16 us (0.958)
  Pallas kernels: 15.9 us -> 15.2 us
    pallas_call x1, Pallas kernels: 14.4 us -> 13.9 us  [shards(): pl.pallas_call(functools.partial(score_kernel, n_img, n_proj, x_size), ou...]
    pallas_call x1, Pallas kernels: 1.58 us -> 1.23 us  [shards(): pl.pallas_call(functools.partial(back_kernel, 2 * img_rows), out_shape=(j...]
where the time goes in v5:
time: 16 us; the launch traced here: 15.8 us
  Pallas kernels  15.2 us (95%)
  between operations  0.64 us (4%)
    pallas_call x1, Pallas kernels, shards(): pl.pallas_call(functools.partial(score_kernel, n_img, n_proj, x_size), ou...  13.9 us
    pallas_call x1, Pallas kernels, shards(): pl.pallas_call(functools.partial(back_kernel, 2 * img_rows), out_shape=(j...  1.23 us

profile of v5, /device:TPU:0, one launch (start us, length us, event | category | flops | bytes accessed | tf_op | source)
XLA Modules:
  0.0 15.8 jit_solution(3099832455724514241)
XLA Ops:
  0.6 13.9 %shard_map.86 = (bf16[320,512]{1,0:T(8,128)(2,1)S(1)}, bf16[512,1024]{1,0:T(8,128)(2,1)S(1)}, bf16[512,1024]{1,0:T(8,128)(2,1)S(1)}, f32[320,1024]{1,0:T(8,128)S...) custom-call(bf16[128,4096]{1,0:T(8,128)(2,1)} %img_hbm.1, bf16[320,4096]{1,0:T(8,128)(2,1)} %proj_hbm.1, ...), custom_call_target="tpu_custom_call" | custom-call | tf_op jit(solution)/shard_map/pallas_call | solution.py:442
  14.6 1.2 %shard_map.87 = (bf16[320,1024]{1,0:T(8,128)(2,1)}, f32[1,128]{1,0:T(1,128)}) custom-call(bf16[320,512]{1,0:T(8,128)(2,1)S(1)} %get-tuple-element.10.posts_ref, bf16[512,1024]{1,0:T(8,128)(2,1)S(1)} %get-tuple-element.11.back_img, bf16[512,1024]{1,0:T(8,128)(2,1)S(1)} %get-tuple-element.12.back_wgt, f32[320,1024]{1,0:T(8,128)S(1)} %get-tuple-element.13.near_img, ...), custom_call_target="tpu_custom_call" | custom-call | tf_op jit(solution)/shard_map/pallas_call | solution.py:477

commit v6 on v5

--- a/solution.py
+++ b/solution.py
@@ -9,8 +9,9 @@
 from jax.sharding import PartitionSpec as P
 
 BLOCK = 32
-PIECES = 2
+PIECES = 1
 PIECE = 16
+DIRECT = 32
 STEP = 256
 LANES = 128
 DEPTH = 512
@@ -81,7 +82,7 @@
     side = lax.rem(odd_x + odd_z, 2)
     beside_x, beside_z = mine + 1 - 2 * odd_x, mine + x_size * (1 - 2 * odd_z)
     beside_xz = beside_x + beside_z - mine
-    quarter = (img_rows - 2 * PIECES * PIECE) // 4
+    quarter = (img_rows - 2 * PIECES * PIECE - DIRECT) // 4
 
     def half_rows(k, n):
         return pl.ds(pl.multiple_of((k * PIECES + n) * PIECE, PIECE), PIECE)
@@ -141,6 +142,7 @@
     with jax.named_scope('greet'):
         lax.fori_loop(0, n_proj, greet_all, 0)
     my_rows = [quarter_rows(odd_x, odd_z)] + [half_rows(side, n) for n in range(PIECES)]
+    my_rows.append(pl.ds(img_rows - DIRECT, DIRECT))
 
     def move_img(t, n):
         slab = pl.ds(pl.multiple_of(img_to(t) * part, LANES), part)
@@ -169,6 +171,8 @@
         for t, n in far:
             move_img(t, n).start()
         near.start()
+        for t in range(2, n_img, 2):
+            move_img(t, PIECES + 1).start()
 
     @pl.when(first_core)
     def _():
@@ -290,6 +294,8 @@
         pass_on(t, n)
     for t in range(2, n_img, 2):
         post_copies[t].start()
+    for t in range(3, n_img, 2):
+        move_img(t, PIECES + 1).start()
 
     term0 = lane + (me * part).astype(jnp.float32)
 
@@ -398,7 +404,7 @@
     def far_bytes(rows):
         return moved.at[pl.ds(2, n_img - 2), pl.ds(0, rows)]
 
-    wait_bytes(far_bytes(PIECES * PIECE + quarter), img_send)
+    wait_bytes(far_bytes(PIECES * PIECE + quarter + DIRECT), img_send)
     with jax.named_scope("quart"):
         wait_bytes(moved.at[pl.ds(2, n_img - 2), pl.ds(0, 3 * quarter)], pass_recv.at[0])
     for t in range(2, n_img):
@@ -409,6 +415,10 @@
     for t in range(2, n_img):
         for rows in half_others:
             take_rows(t, rows)
+    for t in range(2, n_img):
+        with jax.named_scope(f"dir{t}"):
+            move_img(t, PIECES + 1).wait_recv()
+        take_rows(t, my_rows[PIECES + 1])
     wait_bytes(far_bytes(PIECES * PIECE + 3 * quarter), pass_send)
 
 
@@ -467,7 +477,7 @@
             pltpu.VMEM((2, img_rows), f32),
             pltpu.VMEM((n_img * n_proj, 2, img_rows), f32),
             dma((5,)), dma((width // DEPTH // 2,)), dma((width // DEPTH // 2,)), regular, regular,
-            dma((2,)), dma((2,)), dma((2,)), dma, dma((n_img - 2, PIECES + 1)), dma, dma((2,)),
+            dma((2,)), dma((2,)), dma((2,)), dma, dma((n_img - 2, PIECES + 2)), dma, dma((2,)),
             dma, dma((n_img - 1,)), dma, dma,
         ],
         compiler_params=pltpu.CompilerParams(

time: 16 us -> 15.7 us (0.981)
  Pallas kernels: 15.2 us -> 14.9 us
    pallas_call x1, Pallas kernels: 13.9 us -> 13.7 us  [shards(): pl.pallas_call(functools.partial(score_kernel, n_img, n_proj, x_size), ou...]
where the time goes in v6:
time: 15.7 us; the launch traced here: 15.6 us
  Pallas kernels  14.9 us (95%)
  between operations  0.64 us (4%)
    pallas_call x1, Pallas kernels, shards(): pl.pallas_call(functools.partial(score_kernel, n_img, n_proj, x_size), ou...  13.7 us
    pallas_call x1, Pallas kernels, shards(): pl.pallas_call(functools.partial(back_kernel, 2 * img_rows), out_shape=(j...  1.24 us

profile of v6, /device:TPU:0, one launch (start us, length us, event | category | flops | bytes accessed | tf_op | source)
XLA Modules:
  0.0 15.6 jit_solution(4845453624373317124)
XLA Ops:
  0.6 13.7 %shard_map.86 = (bf16[320,512]{1,0:T(8,128)(2,1)S(1)}, bf16[512,1024]{1,0:T(8,128)(2,1)S(1)}, bf16[512,1024]{1,0:T(8,128)(2,1)S(1)}, f32[320,1024]{1,0:T(8,128)S...) custom-call(bf16[128,4096]{1,0:T(8,128)(2,1)} %img_hbm.1, bf16[320,4096]{1,0:T(8,128)(2,1)} %proj_hbm.1, ...), custom_call_target="tpu_custom_call" | custom-call | tf_op jit(solution)/shard_map/pallas_call | solution.py:452
  14.3 1.2 %shard_map.87 = (bf16[320,1024]{1,0:T(8,128)(2,1)}, f32[1,128]{1,0:T(1,128)}) custom-call(bf16[320,512]{1,0:T(8,128)(2,1)S(1)} %get-tuple-element.10.posts_ref, bf16[512,1024]{1,0:T(8,128)(2,1)S(1)} %get-tuple-element.11.back_img, bf16[512,1024]{1,0:T(8,128)(2,1)S(1)} %get-tuple-element.12.back_wgt, f32[320,1024]{1,0:T(8,128)S(1)} %get-tuple-element.13.near_img, ...), custom_call_target="tpu_custom_call" | custom-call | tf_op jit(solution)/shard_map/pallas_call | solution.py:487

commit v7 on v6

--- a/solution.py
+++ b/solution.py
@@ -160,10 +160,12 @@
         src_ref=img_hbm.at[:, pl.ds(pl.multiple_of(img_to(1) * part, LANES), part)], dst_ref=moved.at[1],
         send_sem=near_sem.at[0], recv_sem=near_sem.at[1], device_id={"img": img_to(1)}, device_id_type=MESH)
     small = [pltpu.make_async_remote_copy(
-        src_ref=ref, dst_ref=dst.at[t], send_sem=small_send.at[n], recv_sem=small_recv.at[n],
+        src_ref=ref, dst_ref=dst.at[t], send_sem=small_send, recv_sem=small_recv,
         device_id={"img": img_to(t)}, device_id_type=MESH)
-        for t in range(1, n_img) for n, (ref, dst) in enumerate(((focus_hbm, focus_all), (limit_hbm, limit_all)))]
+        for t in range(1, n_img) for ref, dst in ((focus_hbm, focus_all), (limit_hbm, limit_all))]
     far = [(t, n) for n in range(PIECES + 1) for t in range(2, n_img)]
+
+    small_bytes = noise_ref.at[:, pl.ds(0, 2 * (n_img - 1) * img_rows)]
 
     def send_images():
         for copy in small:
@@ -213,8 +215,7 @@
     def score_chunk(c, slot):
         rows = proj[:, pl.ds(pl.multiple_of(c * DEPTH, DEPTH), DEPTH)]
         got = lax.dot_general(rows, weighted[slot], contract, preferred_element_type=jnp.float32)
-        got = got + lax.dot_general(rows * rows, weighted_sq[slot], contract, preferred_element_type=jnp.float32)
-        total[...] += got
+        return got + lax.dot_general(rows * rows, weighted_sq[slot], contract, preferred_element_type=jnp.float32)
 
     with jax.named_scope("img0"):
         load_img(0).wait()
@@ -231,10 +232,11 @@
                 pl.semaphore_wait(next_token, 1)
             send_images()
 
-        score_chunk(2 * i, 0)
+        got = score_chunk(2 * i, 0)
         terms_chunk(2 * i + 1, 1)
-        score_chunk(2 * i + 1, 1)
+        got = got + score_chunk(2 * i + 1, 1)
         terms_chunk(jnp.minimum(2 * i + 2, width // DEPTH - 1), 0)
+        total[...] += got
         return carry
 
     lax.fori_loop(0, steps, score_step, 0)
@@ -329,8 +331,7 @@
     fill_weights = lambda lo, hi: lax.fori_loop(lo, hi, weights_block, 0)
     fill_weights(0, 1)
     with jax.named_scope("smallx"):
-        for n, every in enumerate((focus_all, limit_all)):
-            wait_bytes(every.at[pl.ds(1, n_img - 1)], small_recv.at[n])
+        wait_bytes(small_bytes, small_recv)
     fill_weights(1, 2)
     fill_weights(2, 2 + per_piece // 2)
     for t, n in far[per_piece:2 * per_piece]:
@@ -398,8 +399,7 @@
     ev_ref[...] = placed
 
     wait_bytes(every_stats.at[pl.ds(1, n_img * n_proj - 1)], stat_send)
-    for n, every in enumerate((focus_all, limit_all)):
-        wait_bytes(every.at[pl.ds(1, n_img - 1)], small_send.at[n])
+    wait_bytes(small_bytes, small_send)
     wait_bytes(every_terms.at[pl.ds(1, n_img - 1)], post_send)
     def far_bytes(rows):
         return moved.at[pl.ds(2, n_img - 2), pl.ds(0, rows)]
@@ -426,18 +426,16 @@
     part = back_img.shape[1]
     steps = part // STEP
     posts = posts_ref[:, near_cols:]
-    last = pltpu.make_async_copy(ev_ref, placed_hbm, out_sem.at[steps])
+    last = pltpu.make_async_copy(ev_ref, placed_hbm, out_sem.at[1])
     last.start()
-    copies = [last]
     for c in range(steps):
         cols = slice(c * STEP, (c + 1) * STEP)
         sums = near_img[:, cols] + jnp.dot(posts, back_img[near_cols:, cols], preferred_element_type=jnp.float32)
         weights = near_wgt[:, cols] + jnp.dot(posts, back_wgt[near_cols:, cols], preferred_element_type=jnp.float32)
         rec[:, cols] = (sums / (weights + 1.0)).astype(jnp.bfloat16)
-        copies.append(pltpu.make_async_copy(rec.at[:, cols], rec_hbm.at[:, cols], out_sem.at[c]))
-        copies[-1].start()
-    for copy in copies:
-        copy.wait()
+        pltpu.make_async_copy(rec.at[:, cols], rec_hbm.at[:, cols], out_sem.at[0]).start()
+    pltpu.make_async_copy(rec, rec_hbm, out_sem.at[0]).wait()
+    last.wait()
 
 
 def shards(n_img, n_proj, images, projections, noise_weight, defocus, orient_count, term_limit, block_plan):
@@ -477,7 +475,7 @@
             pltpu.VMEM((2, img_rows), f32),
             pltpu.VMEM((n_img * n_proj, 2, img_rows), f32),
             dma((5,)), dma((width // DEPTH // 2,)), dma((width // DEPTH // 2,)), regular, regular,
-            dma((2,)), dma((2,)), dma((2,)), dma, dma((n_img - 2, PIECES + 2)), dma, dma((2,)),
+            dma, dma, dma((2,)), dma, dma((n_img - 2, PIECES + 2)), dma, dma((2,)),
             dma, dma((n_img - 1,)), dma, dma,
         ],
         compiler_params=pltpu.CompilerParams(
@@ -489,7 +487,7 @@
         out_shape=(jax.ShapeDtypeStruct((proj_rows, part), bf16), jax.ShapeDtypeStruct((1, img_rows), f32)),
         in_specs=[vmem] * 6,
         out_specs=(hbm, hbm),
-        scratch_shapes=[pltpu.VMEM((proj_rows, part), bf16), dma((part // STEP + 1,))],
+        scratch_shapes=[pltpu.VMEM((proj_rows, part), bf16), dma((2,))],
         compiler_params=pltpu.CompilerParams(vmem_limit_bytes=16 * 1024 * 1024),
     )(*held)
     return reconstruction, evidence.reshape(-1)

time: 15.7 us -> 15.6 us (level)
  no operation moved by 1% of the time
where the time goes in v7:
time: 15.6 us; the launch traced here: 15.4 us
  Pallas kernels  14.8 us (95%)
  between operations  0.64 us (4%)
    pallas_call x1, Pallas kernels, shards(): pl.pallas_call(functools.partial(score_kernel, n_img, n_proj, x_size), ou...  13.6 us
    pallas_call x1, Pallas kernels, shards(): pl.pallas_call(functools.partial(back_kernel, 2 * img_rows), out_shape=(j...  1.21 us

profile of v7, /device:TPU:0, one launch (start us, length us, event | category | flops | bytes accessed | tf_op | source)
XLA Modules:
  0.0 15.4 jit_solution(3476677033119329045)
XLA Ops:
  0.6 13.6 %shard_map.86 = (bf16[320,512]{1,0:T(8,128)(2,1)S(1)}, bf16[512,1024]{1,0:T(8,128)(2,1)S(1)}, bf16[512,1024]{1,0:T(8,128)(2,1)S(1)}, f32[320,1024]{1,0:T(8,128)S...) custom-call(bf16[128,4096]{1,0:T(8,128)(2,1)} %img_hbm.1, bf16[320,4096]{1,0:T(8,128)(2,1)} %proj_hbm.1, ...), custom_call_target="tpu_custom_call" | custom-call | tf_op jit(solution)/shard_map/pallas_call | solution.py:450
  14.2 1.2 %shard_map.87 = (bf16[320,1024]{1,0:T(8,128)(2,1)}, f32[1,128]{1,0:T(1,128)}) custom-call(bf16[320,512]{1,0:T(8,128)(2,1)S(1)} %get-tuple-element.10.posts_ref, bf16[512,1024]{1,0:T(8,128)(2,1)S(1)} %get-tuple-element.11.back_img, bf16[512,1024]{1,0:T(8,128)(2,1)S(1)} %get-tuple-element.12.back_wgt, f32[320,1024]{1,0:T(8,128)S(1)} %get-tuple-element.13.near_img, ...), custom_call_target="tpu_custom_call" | custom-call | tf_op jit(solution)/shard_map/pallas_call | solution.py:485

commit v8 on v7

--- a/solution.py
+++ b/solution.py
@@ -116,9 +116,9 @@
                 signal(all_token, partner, mine)
             pl.when(first_core)(lambda: pl.semaphore_wait(all_token, 1))
 
-    small_loads = [pltpu.make_async_copy(source, target, load_sem.at[n]) for n, (source, target) in enumerate(
-        ((focus_hbm, focus_ref), (limit_hbm, limit_ref), (noise_hbm, noise_ref), (count_hbm, count_ref),
-         (plan_hbm, plan_ref)))]
+    small_loads = [pltpu.make_async_copy(source, target, load_sem.at[n]) for n, source, target in (
+        (0, focus_hbm, focus_ref), (0, limit_hbm, limit_ref), (1, noise_hbm, noise_ref), (2, count_hbm, count_ref),
+        (3, plan_hbm, plan_ref))]
     wide = 2 * DEPTH
     steps = width // wide
 
@@ -184,8 +184,7 @@
         send_images()
 
     with jax.named_scope("small"):
-        small_loads[0].wait()
-        small_loads[1].wait()
+        wait_bytes(focus_all.at[pl.ds(0, 2)], load_sem.at[0])
 
     lane = lax.broadcasted_iota(jnp.int32, (1, LANES), 1).astype(jnp.float32)
     sine[0], sine[1], sine[2] = sine_start(focus_ref[...], lane, width)
@@ -292,10 +291,10 @@
     post_copies[1].start()
 
     per_piece = n_img - 2
+    for t in range(2, n_img, 2):
+        post_copies[t].start()
     for t, n in far[:per_piece]:
         pass_on(t, n)
-    for t in range(2, n_img, 2):
-        post_copies[t].start()
     for t in range(3, n_img, 2):
         move_img(t, PIECES + 1).start()
 
@@ -474,7 +473,7 @@
             pltpu.VMEM((n_img, proj_rows, img_rows), bf16),
             pltpu.VMEM((2, img_rows), f32),
             pltpu.VMEM((n_img * n_proj, 2, img_rows), f32),
-            dma((5,)), dma((width // DEPTH // 2,)), dma((width // DEPTH // 2,)), regular, regular,
+            dma((4,)), dma((width // DEPTH // 2,)), dma((width // DEPTH // 2,)), regular, regular,
             dma, dma, dma((2,)), dma, dma((n_img - 2, PIECES + 2)), dma, dma((2,)),
             dma, dma((n_img - 1,)), dma, dma,
         ],

time: 15.6 us -> 15.6 us (level)
  no operation moved by 1% of the time
where the time goes in v8:
time: 15.6 us; the launch traced here: 15.4 us
  Pallas kernels  14.8 us (95%)
  between operations  0.64 us (4%)
    pallas_call x1, Pallas kernels, shards(): pl.pallas_call(functools.partial(score_kernel, n_img, n_proj, x_size), ou...  13.6 us
    pallas_call x1, Pallas kernels, shards(): pl.pallas_call(functools.partial(back_kernel, 2 * img_rows), out_shape=(j...  1.21 us

profile of v8, /device:TPU:0, one launch (start us, length us, event | category | flops | bytes accessed | tf_op | source)
XLA Modules:
  0.0 15.4 jit_solution(7566488543442012775)
XLA Ops:
  0.6 13.6 %shard_map.86 = (bf16[320,512]{1,0:T(8,128)(2,1)S(1)}, bf16[512,1024]{1,0:T(8,128)(2,1)S(1)}, bf16[512,1024]{1,0:T(8,128)(2,1)S(1)}, f32[320,1024]{1,0:T(8,128)S...) custom-call(bf16[128,4096]{1,0:T(8,128)(2,1)} %img_hbm.1, bf16[320,4096]{1,0:T(8,128)(2,1)} %proj_hbm.1, ...), custom_call_target="tpu_custom_call" | custom-call | tf_op jit(solution)/shard_map/pallas_call | solution.py:449
  14.2 1.2 %shard_map.87 = (bf16[320,1024]{1,0:T(8,128)(2,1)}, f32[1,128]{1,0:T(1,128)}) custom-call(bf16[320,512]{1,0:T(8,128)(2,1)S(1)} %get-tuple-element.10.posts_ref, bf16[512,1024]{1,0:T(8,128)(2,1)S(1)} %get-tuple-element.11.back_img, bf16[512,1024]{1,0:T(8,128)(2,1)S(1)} %get-tuple-element.12.back_wgt, f32[320,1024]{1,0:T(8,128)S(1)} %get-tuple-element.13.near_img, ...), custom_call_target="tpu_custom_call" | custom-call | tf_op jit(solution)/shard_map/pallas_call | solution.py:484
